TPU v7x, 16 devices: a whole 2x2x2 slice. The times are simulated.
16 devices in a mesh: dp: 4 (over z, y), tp: 4 (over x, core).
Axes of the slice: x: 2, y: 2, z: 2, core: 2. Of those that a mesh axis runs over, the one named last changes fastest.
Arguments:
- irreps: bfloat16 [1024, 25, 128], P('dp', None, 'tp')
- norm_gain: float32 [5, 128], P(None, 'tp')
- w_up: bfloat16 [5, 128, 512], P(None, None, 'tp')
- w_gate: bfloat16 [128, 512], P(None, 'tp')
- w_down: bfloat16 [5, 512, 128], P(None, 'tp')
- to_grid: float32 [25, 196], replicated
- from_grid: float32 [196, 24], replicated
- grad_out: bfloat16 [1024, 25, 128], P('dp', None, 'tp')
Outputs:
- output 1: bfloat16 [1024, 25, 128], P('dp', None, 'tp')
- output 2: bfloat16 [1024, 25, 128], P('dp', None, 'tp')
- output 3: bfloat16 [5, 128, 512], P(None, None, 'tp')
- output 4: bfloat16 [128, 512], P(None, 'tp')
- output 5: bfloat16 [5, 512, 128], P(None, 'tp')
All inputs are finite; a program needn't handle non-finite values.
Results may differ from a plain program's by a relative error of at most 0.0126671.
Values are sent between devices in bfloat16 or wider.
A program may use at most 1 GiB of HBM per device.

v0:
```python
import math
import jax
import jax.numpy as jnp
from jax import lax
from jax.sharding import PartitionSpec as P

NORM_EPS = 1e-5


def expand_rows(per_degree):
    return jnp.concatenate([jnp.broadcast_to(per_degree[degree:degree + 1], (2 * degree + 1,) + per_degree.shape[1:]) for degree in range(per_degree.shape[0])], axis=0)


def degree_sums(per_coef):
    degrees = math.isqrt(per_coef.shape[0])
    return jnp.stack([per_coef[degree * degree:(degree + 1) * (degree + 1)].sum(axis=0) for degree in range(degrees)], axis=0)


def silu_grad(pre_act):
    sig_val = jax.nn.sigmoid(pre_act)
    return sig_val * (1.0 + pre_act * (1.0 - sig_val))


def hidden_block(xn_blk, grad_blk, up_rows, gate_loc, down_rows, grid_in, grid_back):
    hidden_act = jnp.einsum('nkc,kch->nkh', xn_blk, up_rows, preferred_element_type=jnp.float32).astype(jnp.bfloat16)
    pre_gate = jnp.dot(xn_blk[:, 0, :], gate_loc, preferred_element_type=jnp.float32).astype(jnp.bfloat16)
    gate_pre_f = pre_gate.astype(jnp.float32)
    gate_val = jax.nn.silu(gate_pre_f).astype(jnp.bfloat16)
    pre_grid = jnp.einsum('nkh,kg->ngh', hidden_act, grid_in, preferred_element_type=jnp.float32).astype(jnp.bfloat16)
    grid_pre_f = pre_grid.astype(jnp.float32)
    grid_val = jax.nn.silu(grid_pre_f).astype(jnp.bfloat16)
    back_proj = jnp.einsum('ngh,gk->nkh', grid_val, grid_back, preferred_element_type=jnp.float32).astype(jnp.bfloat16)
    mixed_act = jnp.concatenate([gate_val[:, None, :], back_proj], axis=1)
    part_out = jnp.einsum('nkh,khc->nkc', mixed_act, down_rows, preferred_element_type=jnp.float32).astype(jnp.bfloat16)
    d_mixed = jnp.einsum('nkc,khc->nkh', grad_blk, down_rows, preferred_element_type=jnp.float32).astype(jnp.bfloat16)
    g_down = jnp.einsum('nkh,nkc->khc', mixed_act, grad_blk, preferred_element_type=jnp.float32)
    d_grid = jnp.einsum('nkh,gk->ngh', d_mixed[:, 1:, :], grid_back, preferred_element_type=jnp.float32).astype(jnp.bfloat16)
    d_pre_grid = (d_grid.astype(jnp.float32) * silu_grad(grid_pre_f)).astype(jnp.bfloat16)
    d_hidden = jnp.einsum('ngh,kg->nkh', d_pre_grid, grid_in, preferred_element_type=jnp.float32).astype(jnp.bfloat16)
    d_pre_gate = (d_mixed[:, 0, :].astype(jnp.float32) * silu_grad(gate_pre_f)).astype(jnp.bfloat16)
    g_up = jnp.einsum('nkc,nkh->kch', xn_blk, d_hidden, preferred_element_type=jnp.float32)
    g_gate = jnp.einsum('nc,nh->ch', xn_blk[:, 0, :], d_pre_gate, preferred_element_type=jnp.float32)
    d_xn = jnp.einsum('nkh,kch->nkc', d_hidden, up_rows, preferred_element_type=jnp.float32)
    d_xn_zero = d_xn[:, 0, :] + jnp.einsum('nh,ch->nc', d_pre_gate, gate_loc, preferred_element_type=jnp.float32)
    d_xn = jnp.concatenate([d_xn_zero[:, None, :], d_xn[:, 1:, :]], axis=1).astype(jnp.bfloat16)
    return part_out, d_xn, g_up, g_gate, g_down


def hidden_pass(xn_full, grad_full, up_loc, gate_loc, down_loc, to_grid, from_grid):
    node_count, coef_count, channels = xn_full.shape
    blk_rows = math.gcd(node_count, 128)
    blk_count = node_count // blk_rows
    up_rows = expand_rows(up_loc)
    down_rows = expand_rows(down_loc)
    grid_in = to_grid.astype(jnp.bfloat16)
    grid_back = from_grid.astype(jnp.bfloat16)

    def scan_step(grad_sums, blk_pair):
        part_out, d_xn, g_up, g_gate, g_down = hidden_block(blk_pair[0], blk_pair[1], up_rows, gate_loc, down_rows, grid_in, grid_back)
        return (grad_sums[0] + g_up, grad_sums[1] + g_gate, grad_sums[2] + g_down), (part_out, d_xn)

    init_sums = (jnp.zeros(up_rows.shape, jnp.float32), jnp.zeros(gate_loc.shape, jnp.float32), jnp.zeros(down_rows.shape, jnp.float32))
    blk_shape = (blk_count, blk_rows, coef_count, channels)
    total_sums, (part_outs, d_xns) = lax.scan(scan_step, init_sums, (xn_full.reshape(blk_shape), grad_full.reshape(blk_shape)))
    full_shape = (node_count, coef_count, channels)
    return part_outs.reshape(full_shape), d_xns.reshape(full_shape), degree_sums(total_sums[0]), total_sums[1], degree_sums(total_sums[2])


def solution(mesh):
    tp_size = mesh.shape['tp']
    act_spec = P('dp', None, 'tp')
    in_specs = (act_spec, P(None, 'tp'), P(None, None, 'tp'), P(None, 'tp'), P(None, 'tp', None), P(None, None), P(None, None), act_spec)
    out_specs = (act_spec, act_spec, P(None, None, 'tp'), P(None, 'tp'), P(None, 'tp', None))

    def local_step(x_loc, gain_loc, up_loc, gate_loc, down_loc, to_grid, from_grid, grad_loc):
        coef_count = x_loc.shape[1]
        channels = x_loc.shape[2] * tp_size
        vec_count = channels * (coef_count - 1)
        x_f = x_loc.astype(jnp.float32)
        scalar = x_f[:, 0, :]
        vector = x_f[:, 1:, :]
        node_stats = jnp.stack([jnp.sum(scalar, axis=-1), jnp.sum(scalar * scalar, axis=-1), jnp.sum(vector * vector, axis=(1, 2))], axis=-1)
        node_stats = lax.psum(node_stats, 'tp')
        mean_s = node_stats[:, 0:1] / channels
        inv_s = lax.rsqrt(node_stats[:, 1:2] / channels - mean_s * mean_s + NORM_EPS)
        inv_v = lax.rsqrt(node_stats[:, 2] / vec_count + NORM_EPS)[:, None, None]
        hat_s = (scalar - mean_s) * inv_s
        hat_v = vector * inv_v
        gain_rows = expand_rows(gain_loc)
        xn_loc = jnp.concatenate([(hat_s * gain_rows[0])[:, None, :], hat_v * gain_rows[1:]], axis=1).astype(jnp.bfloat16)
        xn_full = lax.all_gather(xn_loc, 'tp', axis=2, tiled=True)
        grad_full = lax.all_gather(grad_loc, 'tp', axis=2, tiled=True)
        part_out, d_xn_part, g_up, g_gate, g_down = hidden_pass(xn_full, grad_full, up_loc, gate_loc, down_loc, to_grid, from_grid)
        ffn_delta = lax.psum_scatter(part_out, 'tp', scatter_dimension=2, tiled=True)
        out_loc = (x_f + ffn_delta.astype(jnp.float32)).astype(jnp.bfloat16)
        d_norm = lax.psum_scatter(d_xn_part, 'tp', scatter_dimension=2, tiled=True).astype(jnp.float32)
        d_hat_s = d_norm[:, 0, :] * gain_rows[0]
        d_hat_v = d_norm[:, 1:, :] * gain_rows[1:]
        back_stats = jnp.stack([jnp.sum(d_hat_s, axis=-1), jnp.sum(d_hat_s * hat_s, axis=-1), jnp.sum(d_hat_v * vector, axis=(1, 2))], axis=-1)
        back_stats = lax.psum(back_stats, 'tp')
        dx_s = inv_s * (d_hat_s - back_stats[:, 0:1] / channels - hat_s * back_stats[:, 1:2] / channels)
        dx_v = inv_v * d_hat_v - vector * (inv_v ** 3) * (back_stats[:, 2] / vec_count)[:, None, None]
        d_irreps = (jnp.concatenate([dx_s[:, None, :], dx_v], axis=1) + grad_loc.astype(jnp.float32)).astype(jnp.bfloat16)
        d_up = lax.psum(g_up, 'dp').astype(jnp.bfloat16)
        d_gate = lax.psum(g_gate, 'dp').astype(jnp.bfloat16)
        d_down = lax.psum(g_down, 'dp').astype(jnp.bfloat16)
        return out_loc, d_irreps, d_up, d_gate, d_down

    return jax.shard_map(local_step, mesh=mesh, in_specs=in_specs, out_specs=out_specs, check_vma=False)
```

profile of v0, /device:TPU:0, one launch (start us, length us, event | category | flops | bytes accessed | tf_op | source)
XLA Modules:
  0.0 198.0 jit_solution(14386671694306684822)
XLA Ops:
  7.2 1.1 convert_element_type.116
  8.6 8.8 %psum.35 = f32[256,3]{0,1:T(4,128)S(1)} all-reduce(f32[256,3]{0,1:T(4,128)S(1)} %pad_maximum_fusion.3), channel_id=1, replica_groups=mesh['dp'=4,'tp'=4] {'tp'}, use_global_device_ids=true, to_apply=%region_3.0 | all-reduce | flops 768 | bytes 6144 | tf_op jit(solution)/shard_map/psum | solution.py:83
  20.6 16.7 %all-gather.3.cloned.1.call-done = bf16[256,25,128]{0,2,1:T(8,128)(2,1)} async-done(((bf16[256,25,32]{0,2,1:T(8,128)(2,1)}), bf16[256,25,128]{0,2,1:T(8,128)(2,1)}) %all-gather.3.cloned.1.call-update) | async-done | bytes 1638416 | tf_op jit(solution)/shard_map/all_gather | solution.py:91
  37.3 3.5 %reshape.141 = bf16[2,128,25,128]{1,0,3,2:T(2,128)(2,1)S(1)} reshape(bf16[256,25,128]{0,2,1:T(8,128)(2,1)} %all-gather.3.cloned.1.call-done) | data formatting | bytes 3276800 | tf_op jit(solution)/shard_map/reshape | solution.py:64
  40.8 3.6 %copy.40 = bf16[2,128,25,128]{3,1,2,0:T(8,128)(2,1)} copy(bf16[2,128,25,128]{1,0,3,2:T(2,128)(2,1)S(1)} %reshape.141) | data formatting | bytes 3276800
  44.4 12.4 %all-gather.5.cloned.1.call-done = bf16[256,25,128]{0,2,1:T(8,128)(2,1)} async-done(((bf16[256,25,32]{0,2,1:T(8,128)(2,1)}), bf16[256,25,128]{0,2,1:T(8,128)(2,1)}) %all-gather.5.cloned.1.call-update) | async-done | bytes 1638416 | tf_op jit(solution)/shard_map/all_gather | solution.py:92
  56.8 3.7 %copy.39 = bf16[256,25,128]{2,0,1:T(8,128)(2,1)} copy(bf16[256,25,128]{0,2,1:T(8,128)(2,1)} %all-gather.5.cloned.1.call-done) | data formatting | bytes 3276800 | tf_op jit(solution)/shard_map/all_gather | solution.py:92
  60.5 70.7 %while.19 = (s32[]{:T(128)}, f32[25,128,128]{2,1,0:T(8,128)}, f32[128,128]{1,0:T(8,128)S(1)}, f32[25,128,128]{2,1,0:T(8,128)}, bf16[2,128,25,128]{3,1,2,0:T(8,12...) while((s32[]{:T(128)}, f32[25,128,128]{2,1,0:T(8,128)}, ...), condition=%wide.region_5.6_spmd.clone, body=%wide.region_4.5_spmd.clone.sunk | while | flops 1339604992 | bytes 121116680 | solution.py:64
  60.5 1.3 dynamic-slice_bitcast_fusion.2
  63.1 1.0 slice.271
  64.4 4.6 %convolution_convert_fusion.7 = bf16[128,128,196]{1,2,0:T(8,128)(2,1)} fusion(bf16[128,25,128]{2,0,1:T(8,128)(2,1)S(1)} %fusion.123, bf16[25,196]{1,0:T(8,128)(2,1)S(1)} %get-tuple-element.336), kind=kOutput, calls=%fused_computation.12.clone.1 | convolution fusion | flops 163774464 | bytes 7251528 | tf_op jit(solution)/shard_map/while/body/eval_jaxpr/nkh,kg->ngh/dot_general | solution.py:29
  69.0 10.6 %fusion.125 = bf16[128,25,128]{2,1,0:T(8,128)(2,1)} fusion(bf16[128,128,196]{1,2,0:T(8,128)(2,1)} %convolution_convert_fusion.7, bf16[128,24,128]{2,0,1:T(8,128)(2,1)} %slice.271, bf16[25,196]{1,0:T(8,128)(2,1)S(1)} %get-tuple-element.336, bf16[196,24]{0,1:T(8,128)(2,1)S(1)} %get-tuple-element.334), kind=kOutput, calls=%fused_computation.24.clone.1 | convolution fusion | flops 353648640 | bytes 8047368 | tf_op jit(solution)/shard_map/while/body/eval_jaxpr/ngh,kg->nkh/dot_general | solution.py:39
  79.7 6.5 %fusion.127 = bf16[128,24,128]{2,1,0:T(8,128)(2,1)S(1)} fusion(bf16[128,128,196]{1,2,0:T(8,128)(2,1)} %convolution_convert_fusion.7, bf16[196,24]{0,1:T(8,128)(2,1)S(1)} %get-tuple-element.334), kind=kOutput, calls=%fused_computation.29.clone.1 | convolution fusion | flops 173801472 | bytes 7218368 | tf_op jit(solution)/shard_map/while/body/eval_jaxpr/ngh,gk->nkh/dot_general | solution.py:32
  87.4 0.9 select_add_fusion.4
  92.6 0.8 copy-done.13
  94.7 1.2 copy-done.14
  95.8 1.3 dynamic-slice_bitcast_fusion.2
  98.4 1.0 slice.271
  99.8 4.6 %convolution_convert_fusion.7 = bf16[128,128,196]{1,2,0:T(8,128)(2,1)} fusion(bf16[128,25,128]{2,0,1:T(8,128)(2,1)S(1)} %fusion.123, bf16[25,196]{1,0:T(8,128)(2,1)S(1)} %get-tuple-element.336), kind=kOutput, calls=%fused_computation.12.clone.1 | convolution fusion | flops 163774464 | bytes 7251528 | tf_op jit(solution)/shard_map/while/body/eval_jaxpr/nkh,kg->ngh/dot_general | solution.py:29
  104.4 10.6 %fusion.125 = bf16[128,25,128]{2,1,0:T(8,128)(2,1)} fusion(bf16[128,128,196]{1,2,0:T(8,128)(2,1)} %convolution_convert_fusion.7, bf16[128,24,128]{2,0,1:T(8,128)(2,1)} %slice.271, bf16[25,196]{1,0:T(8,128)(2,1)S(1)} %get-tuple-element.336, bf16[196,24]{0,1:T(8,128)(2,1)S(1)} %get-tuple-element.334), kind=kOutput, calls=%fused_computation.24.clone.1 | convolution fusion | flops 353648640 | bytes 8047368 | tf_op jit(solution)/shard_map/while/body/eval_jaxpr/ngh,kg->nkh/dot_general | solution.py:39
  115.0 6.5 %fusion.127 = bf16[128,24,128]{2,1,0:T(8,128)(2,1)S(1)} fusion(bf16[128,128,196]{1,2,0:T(8,128)(2,1)} %convolution_convert_fusion.7, bf16[196,24]{0,1:T(8,128)(2,1)S(1)} %get-tuple-element.334), kind=kOutput, calls=%fused_computation.29.clone.1 | convolution fusion | flops 173801472 | bytes 7218368 | tf_op jit(solution)/shard_map/while/body/eval_jaxpr/ngh,gk->nkh/dot_general | solution.py:32
  122.8 0.9 select_add_fusion.4
  130.0 1.2 copy-done.14
  131.2 4.6 %copy.43 = bf16[2,128,25,128]{1,0,3,2:T(2,128)(2,1)S(1)} copy(bf16[2,128,25,128]{3,1,2,0:T(8,128)(2,1)} %get-tuple-element.77) | data formatting | bytes 3276800 | tf_op jit(solution)/shard_map/while | solution.py:64
  135.8 2.0 reshape.144
  139.3 2.1 %copy.42 = bf16[2,128,25,128]{1,0,3,2:T(2,128)(2,1)S(1)} copy(bf16[2,128,25,128]{3,1,2,0:T(8,128)(2,1)S(1)} %copy-done.15) | data formatting | bytes 3276800 | tf_op jit(solution)/shard_map/while | solution.py:64
  141.3 2.0 reshape.143
  146.9 33.6 %all-reduce.2 = (bf16[5,128,128]{2,1,0:T(8,128)(2,1)}, bf16[128,128]{1,0:T(8,128)(2,1)}, bf16[5,128,128]{2,1,0:T(8,128)(2,1)}) all-reduce(f32[5,128,128]{2,1,0:T(8,128)} %bitcast_dynamic-update-slice_fusion.4, f32[128,128]{1,0:T(8,128)S(1)} %get-tuple-element.79, ...), channel_id=1, replica_groups=mesh['dp'=4,'tp'=4] {'dp'}, use_global_device_ids=true, to_apply=%region_16.17 | all-reduce | flops 180224 | bytes 1081344 | tf_op jit(solution)/shard_map/psum | solution.py:104
  180.5 1.1 convert_element_type.121
  181.9 6.4 %psum.36 = f32[256,3]{0,1:T(4,128)S(1)} all-reduce(f32[256,3]{0,1:T(4,128)S(1)} %pad_maximum_fusion.4), channel_id=1, replica_groups=mesh['dp'=4,'tp'=4] {'tp'}, use_global_device_ids=true, to_apply=%region_11.12 | all-reduce | flops 768 | bytes 6144 | tf_op jit(solution)/shard_map/psum | solution.py:100
  188.5 0.9 fusion.51
  189.6 1.9 add_convert_fusion
  (178 shorter events, 26.3 us)
Async XLA Ops:
  7.2 30.2 %all-gather.3.cloned.1.call-start = ((), (), s32[]{:S(2)}) async-start(), calls=%async_computation.2 | async-start | bytes 2048000 | tf_op jit(solution)/shard_map/all_gather | solution.py:91
  8.3 10.8 %copy-start.9 = (f32[256,25,32]{0,2,1:T(8,128)}, f32[256,25,32]{0,2,1:T(8,128)S(1)}, u32[]{:S(2)}) copy-start(f32[256,25,32]{0,2,1:T(8,128)S(1)} %convert_element_type.116) | copy-start | bytes 2457604
  8.5 11.5 %copy-start.24 = (f32[196,24]{0,1:T(8,128)S(1)}, f32[196,24]{0,1:T(8,128)}, u32[]{:S(2)}) copy-start(f32[196,24]{0,1:T(8,128)} %param.16) | copy-start | bytes 56452
  8.5 11.5 %copy-start.23 = (f32[25,196]{1,0:T(8,128)S(1)}, f32[25,196]{1,0:T(8,128)}, u32[]{:S(2)}) copy-start(f32[25,196]{1,0:T(8,128)} %param.15) | copy-start | bytes 58804
  8.5 11.5 %copy-start.21 = (bf16[5,128,128]{2,1,0:T(8,128)(2,1)S(1)}, bf16[5,128,128]{2,1,0:T(8,128)(2,1)}, u32[]{:S(2)}) copy-start(bf16[5,128,128]{2,1,0:T(8,128)(2,1)} %param.12) | copy-start | bytes 491524
  8.5 11.5 %copy-start.31 = (f32[32]{0:T(128)}, f32[32]{0:T(128)S(1)}, u32[]{:S(2)}) copy-start(f32[32]{0:T(128)S(1)} %get-tuple-element.209) | copy-start | bytes 388
  17.4 2.7 %copy-start.27 = (f32[256,1]{0,1:T(1,128)}, f32[256,1]{0,1:T(1,128)S(1)}, u32[]{:S(2)}) copy-start(f32[256,1]{0,1:T(1,128)S(1)} %get-tuple-element.206) | copy-start | bytes 3076
  17.4 2.7 %copy-start.29 = (f32[256,1]{0,1:T(1,128)}, f32[256,1]{0,1:T(1,128)S(1)}, u32[]{:S(2)}) copy-start(f32[256,1]{0,1:T(1,128)S(1)} %get-tuple-element.208) | copy-start | bytes 3076
  18.0 2.1 %copy-start.22 = (bf16[5,128,128]{2,1,0:T(8,128)(2,1)S(1)}, bf16[5,128,128]{2,1,0:T(8,128)(2,1)}, u32[]{:S(2)}) copy-start(bf16[5,128,128]{2,1,0:T(8,128)(2,1)} %param.14) | copy-start | bytes 491524
  19.1 37.7 %all-gather.5.cloned.1.call-start = ((), (), s32[]{:S(2)}) async-start(), calls=%async_computation.3 | async-start | bytes 2048000 | tf_op jit(solution)/shard_map/all_gather | solution.py:92
  19.9 160.6 %reduce-scatter.5.cloned.1.call-start = ((), (), s32[]{:S(2)}) async-start(), calls=%async_computation.5 | async-start | bytes 2048000 | tf_op jit(solution)/shard_map/reduce_scatter | solution.py:96
  44.4 16.1 %copy-start.18 = (bf16[128,128]{1,0:T(8,128)(2,1)S(1)}, bf16[128,128]{1,0:T(8,128)(2,1)}, u32[]{:S(2)}) copy-start(bf16[128,128]{1,0:T(8,128)(2,1)} %param.13) | copy-start | bytes 98308
  60.5 1.7 copy-start.4
  79.7 7.0 %copy-start.1 = (f32[25,128,128]{2,1,0:T(8,128)S(1)}, f32[25,128,128]{2,1,0:T(8,128)}, u32[]{:S(2)}) copy-start(f32[25,128,128]{2,1,0:T(8,128)} %get-tuple-element.311) | copy-start | bytes 4915204 | tf_op jit(solution)/shard_map/while
  88.3 2.0 %copy-start.11 = (bf16[2,128,25,128]{3,1,2,0:T(8,128)(2,1)S(1)}, bf16[2,128,25,128]{3,1,2,0:T(8,128)(2,1)}, u32[]{:S(2)}) copy-start(bf16[2,128,25,128]{3,1,2,0:T(8,128)(2,1)} %get-tuple-element.315) | copy-start | bytes 4915204 | tf_op jit(solution)/shard_map/while
  89.0 1.8 copy-start.6
  89.5 2.0 %copy-start.5 = (bf16[2,128,25,128]{3,1,0,2:T(8,128)(2,1)S(1)}, bf16[2,128,25,128]{3,1,0,2:T(8,128)(2,1)}, u32[]{:S(2)}) copy-start(bf16[2,128,25,128]{3,1,0,2:T(8,128)(2,1)} %get-tuple-element.332) | copy-start | bytes 4915204 | tf_op jit(solution)/shard_map/while
  91.5 2.0 %copy-start.13 = (bf16[2,128,25,128]{3,1,2,0:T(8,128)(2,1)S(1)}, bf16[2,128,25,128]{3,1,2,0:T(8,128)(2,1)}, u32[]{:S(2)}) copy-start(bf16[2,128,25,128]{3,1,2,0:T(8,128)(2,1)} %get-tuple-element.314) | copy-start | bytes 4915204 | tf_op jit(solution)/shard_map/while
  115.0 7.0 %copy-start.1 = (f32[25,128,128]{2,1,0:T(8,128)S(1)}, f32[25,128,128]{2,1,0:T(8,128)}, u32[]{:S(2)}) copy-start(f32[25,128,128]{2,1,0:T(8,128)} %get-tuple-element.311) | copy-start | bytes 4915204 | tf_op jit(solution)/shard_map/while
  123.7 2.0 %copy-start.11 = (bf16[2,128,25,128]{3,1,2,0:T(8,128)(2,1)S(1)}, bf16[2,128,25,128]{3,1,2,0:T(8,128)(2,1)}, u32[]{:S(2)}) copy-start(bf16[2,128,25,128]{3,1,2,0:T(8,128)(2,1)} %get-tuple-element.315) | copy-start | bytes 4915204 | tf_op jit(solution)/shard_map/while
  124.4 1.8 copy-start.6
  124.8 2.0 %copy-start.5 = (bf16[2,128,25,128]{3,1,0,2:T(8,128)(2,1)S(1)}, bf16[2,128,25,128]{3,1,0,2:T(8,128)(2,1)}, u32[]{:S(2)}) copy-start(bf16[2,128,25,128]{3,1,0,2:T(8,128)(2,1)} %get-tuple-element.332) | copy-start | bytes 4915204 | tf_op jit(solution)/shard_map/while
  126.8 2.0 %copy-start.13 = (bf16[2,128,25,128]{3,1,2,0:T(8,128)(2,1)S(1)}, bf16[2,128,25,128]{3,1,2,0:T(8,128)(2,1)}, u32[]{:S(2)}) copy-start(bf16[2,128,25,128]{3,1,2,0:T(8,128)(2,1)} %get-tuple-element.314) | copy-start | bytes 4915204 | tf_op jit(solution)/shard_map/while
  137.8 51.8 %reduce-scatter.3.cloned.1.call-start = ((), (), s32[]{:S(2)}) async-start(), calls=%async_computation.4 | async-start | bytes 2048000 | tf_op jit(solution)/shard_map/reduce_scatter | solution.py:94
  141.3 2.0 %copy-start.3 = (f32[25,128,128]{2,1,0:T(8,128)S(1)}, f32[25,128,128]{2,1,0:T(8,128)}, u32[]{:S(2)}) copy-start(f32[25,128,128]{2,1,0:T(8,128)} %get-tuple-element.78) | copy-start | bytes 4915204
  143.4 3.3 %copy-start.8 = (f32[25,128,128]{2,1,0:T(8,128)S(1)}, f32[25,128,128]{2,1,0:T(8,128)}, u32[]{:S(2)}) copy-start(f32[25,128,128]{2,1,0:T(8,128)} %get-tuple-element.80) | copy-start | bytes 4915204
  146.7 34.8 %copy-start.10 = (f32[256,25,32]{0,2,1:T(8,128)S(1)}, f32[256,25,32]{0,2,1:T(8,128)}, u32[]{:S(2)}) copy-start(f32[256,25,32]{0,2,1:T(8,128)} %copy-done.9) | copy-start | bytes 2457604
  146.7 34.8 %copy-start.28 = (f32[256,1]{0,1:T(1,128)S(1)}, f32[256,1]{0,1:T(1,128)}, u32[]{:S(2)}) copy-start(f32[256,1]{0,1:T(1,128)} %copy-done.27) | copy-start | bytes 3076
  146.7 34.8 %copy-start.30 = (f32[256,1]{0,1:T(1,128)S(1)}, f32[256,1]{0,1:T(1,128)}, u32[]{:S(2)}) copy-start(f32[256,1]{0,1:T(1,128)} %copy-done.29) | copy-start | bytes 3076
  146.8 34.8 %copy-start.32 = (f32[32]{0:T(128)S(1)}, f32[32]{0:T(128)}, u32[]{:S(2)}) copy-start(f32[32]{0:T(128)} %copy-done.31) | copy-start | bytes 388
  146.8 34.9 %copy-start.20 = (f32[24,32]{1,0:T(8,128)S(1)}, f32[24,32]{1,0:T(8,128)}, u32[]{:S(2)}) copy-start(f32[24,32]{1,0:T(8,128)} %copy-done.19) | copy-start | bytes 9220
  181.9 6.7 %copy-start.16 = (bf16[256,25,32]{0,2,1:T(8,128)(2,1)S(1)}, bf16[256,25,32]{0,2,1:T(8,128)(2,1)}, u32[]{:S(2)}) copy-start(bf16[256,25,32]{0,2,1:T(8,128)(2,1)} %param.17) | copy-start | bytes 1228804
  (17 other events, 19.8 us)
Sparse Core Ops, SparseCore 0:
  19.2 18.0 all-gather.2
  38.9 17.8 all-gather.4
  138.0 24.5 reduce-scatter.4
  164.9 24.6 reduce-scatter.2
where the time goes:
time: 199 us; the launch traced here: 198 us
  matrix products  52.8 us (27%)
  blocking collectives  48.7 us (24%)
  local copies, waits for them, and re-layouts  43.6 us (22%)
  waiting for transfers between devices  30.1 us (15%)
  between operations  14.4 us (7%)
  other arithmetic  8.12 us (4%)
    psum x1, blocking collectives, local_step(): d_up = lax.psum(g_up, 'dp').astype(jnp.bfloat16)  33.6 us
    dot_general x2, matrix products, hidden_block(): jnp.einsum('ngh,kg->nkh', d_pre_grid, grid_in, preferred_element_type=jnp...  21.3 us
    all_gather x1, waiting for transfers between devices, local_step(): xn_full = lax.all_gather(xn_loc, 'tp', axis=2, tiled=True)  16.7 us
    dot_general x2, matrix products, hidden_block(): jnp.einsum('ngh,gk->nkh', grid_val, grid_back, preferred_element_type=jnp...  13 us
    all_gather x1, waiting for transfers between devices, local_step(): grad_full = lax.all_gather(grad_loc, 'tp', axis=2, tiled=True)  12.4 us
    while x44, local copies, waits for them, and re-layouts  11.6 us
    dot_general x2, matrix products, hidden_block(): jnp.einsum('nkh,kg->ngh', hidden_act, grid_in, preferred_element_type=jnp...  9.29 us
    psum x1, blocking collectives, local_step(): node_stats = lax.psum(node_stats, 'tp')  8.77 us
  transfers between devices with their start and end apart: 4, of which 3 were waited for; matrix products, arithmetic and copies ran while one was open for 9% of the time, Pallas kernels for 0%

commit v1 on v0

v1 whole, which is shorter than its diff:
```python
import functools
import math
import jax
import jax.numpy as jnp
from jax import lax
from jax.experimental import pallas as pl
from jax.experimental.pallas import tpu as pltpu
from jax.sharding import PartitionSpec as P

NORM_EPS = 1e-5
F32 = jnp.float32
BF16 = jnp.bfloat16
MESH = pl.DeviceIdType.MESH
LANES = 128
SUB = 8
KPAD = 256


def mm(lhs, rhs):
    return jnp.dot(lhs, rhs, preferred_element_type=F32)


def mm_nt(lhs, rhs):
    return lax.dot_general(lhs, rhs, (((1,), (1,)), ((), ())), preferred_element_type=F32)


def degree_span(degree):
    return range(degree * degree, (degree + 1) * (degree + 1))


def lane_cat(ref, chunk, degree):
    parts = [ref[chunk, coef] for coef in degree_span(degree)]
    return parts[0] if len(parts) == 1 else jnp.concatenate(parts, axis=1)


def pair_rows(first, second):
    groups = first.shape[0] // SUB
    shape = (groups, SUB, first.shape[1])
    return jnp.concatenate([first.reshape(shape), second.reshape(shape)], axis=1).astype(BF16)


def split_coefs(per_degree):
    out = []
    for degree, value in enumerate(per_degree):
        out += [value[:, LANES * j:LANES * (j + 1)] for j in range(2 * degree + 1)]
    return out


def rounded(value):
    return value.astype(BF16).astype(F32)


def iota2(shape, axis):
    return lax.broadcasted_iota(jnp.int32, shape, axis)


def ones_where(cond):
    return jnp.where(cond, 1.0, 0.0).astype(BF16)


def dp_peer(hop):
    dp = lax.axis_index('dp')
    zpos, ypos = dp // 2, dp % 2
    if hop % 2:
        ypos = 1 - ypos
    if hop // 2:
        zpos = 1 - zpos
    return zpos * 2 + ypos


def tp_peer(hop):
    tp = lax.axis_index('tp')
    xpos, core = tp // 2, tp % 2
    if hop % 2:
        core = 1 - core
    if hop // 2:
        xpos = 1 - xpos
    return xpos * 2 + core


def chan_rows(tp, chan_loc):
    return pl.ds(pl.multiple_of(tp * chan_loc, chan_loc), chan_loc)


def build_grid_mats(to_ref, fromt_ref, up_mat, dgrid_mat, z_mat, dh_mat, blk_pts):
    coefs, points = to_ref.shape
    vecs = fromt_ref.shape[0]
    blk_rows = blk_pts * SUB
    to_b = to_ref[...].astype(BF16)
    from_b = fromt_ref[...].astype(BF16)

    def spread(count, shape, axis):
        return ones_where(iota2(shape, axis) // SUB == iota2(shape, 1 - axis))

    to_cols = lax.dot_general(to_b, spread(coefs, (coefs, KPAD), 1), (((0,), (0,)), ((), ())), preferred_element_type=F32)
    from_cols = lax.dot_general(from_b, spread(vecs, (vecs, KPAD), 1), (((0,), (0,)), ((), ())), preferred_element_type=F32)
    to_cols = (to_cols * 0.5).astype(BF16)
    from_cols = (from_cols * 0.5).astype(BF16)
    to_rows = mm(spread(coefs, (dh_mat.shape[1], coefs), 0), to_b).astype(BF16)
    from_rows = mm(spread(vecs, (z_mat.shape[1], vecs), 0), from_b).astype(BF16)

    def diagonal(value):
        same = iota2(value.shape, 0) % SUB == iota2(value.shape, 1) % SUB
        return jnp.where(same, value, 0.0).astype(BF16)

    def blk_step(blk, carry):
        first = blk * blk_pts
        shape = (blk_rows, points)
        pick = ones_where(iota2(shape, 0) // SUB + first == iota2(shape, 1))
        shape = (points, KPAD)
        col = iota2(shape, 1)
        pick_t = ones_where((col // SUB + first == iota2(shape, 0)) & (col < blk_rows))
        up_mat[blk] = diagonal(mm(pick, to_cols))
        dgrid_mat[blk] = diagonal(mm(pick, from_cols))
        z_mat[blk] = diagonal(mm(from_rows, pick_t))
        dh_mat[blk] = diagonal(mm(to_rows, pick_t))
        return carry

    lax.fori_loop(0, points // blk_pts, blk_step, 0)


def kernel(dims, x_ref, g_ref, gain_ref, up_ref, gate_ref, down_ref, to_ref, fromt_ref,
           out_ref, dx_ref, dup_ref, dgate_ref, ddown_ref,
           xfull, gfull, nfull, gain_rx, gain_cols, up_t, down_t, gate_t,
           up_mat, dgrid_mat, z_mat, dh_mat, ybuf, dmbuf, dgbuf, dm_zero, mbuf, dhbuf, dpg_buf,
           stat_buf, part, rs1, rs2_src, rs2, back_src, back_rx, wgrad, wgrad_rx, wsum, wfull,
           ag_ss, ag_rs, gain_ss, gain_rs, rs1_ss, rs1_rs, rs2_ss, rs2_rs, back_ss, back_rs, w1_ss, w1_rs, w2_ss, w2_rs):
    coefs, chan_loc, _ = x_ref.shape
    degrees = gain_ref.shape[0]
    channels = chan_loc * 4
    vec_count = channels * (coefs - 1)
    hidden = gate_ref.shape[1]
    chunks = dims['chunks']
    blk_count = up_mat.shape[0]
    blk_rows = up_mat.shape[1]
    steps = hidden // SUB // 2
    quarter = wgrad.shape[0] // 4
    me = lax.axis_index('tp')
    my_dp = lax.axis_index('dp')
    sources = (g_ref, x_ref)
    fulls = (gfull, xfull)
    grad, feat = 0, 1
    dxs, outs = 0, 1
    copies = {}

    def send(key, src, dst, ssem, rsem, axis, peer):
        copy = pltpu.make_async_remote_copy(src_ref=src, dst_ref=dst, send_sem=ssem, recv_sem=rsem, device_id={axis: peer}, device_id_type=MESH)
        copy.start()
        copies[key] = copy

    def lanes_of(chunk):
        return pl.ds(chunk * LANES, LANES)

    barrier = pltpu.get_barrier_semaphore()
    for hop in (1, 2, 3):
        pl.semaphore_signal(barrier, inc=1, device_id={'tp': tp_peer(hop)}, device_id_type=MESH)
        pl.semaphore_signal(barrier, inc=1, device_id={'dp': dp_peer(hop)}, device_id_type=MESH)
    pl.semaphore_wait(barrier, 6)

    for hop in (1, 2, 3):
        send(('gain', hop), gain_ref, gain_rx.at[hop - 1], gain_ss.at[hop - 1], gain_rs.at[hop - 1], 'tp', tp_peer(hop))
    for chunk in range(chunks):
        for arr in (grad, feat):
            for hop in (2, 1):
                send(('ag', arr, chunk, hop), sources[arr].at[:, :, lanes_of(chunk)], fulls[arr].at[chunk, :, chan_rows(me, chan_loc), :],
                     ag_ss.at[arr, chunk, hop - 1], ag_rs.at[arr, chunk, hop - 1], 'tp', tp_peer(hop))

    def relay(arr, chunk):
        copies[('ag', arr, chunk, 2)].wait_recv()
        block = fulls[arr].at[chunk, :, chan_rows(tp_peer(2), chan_loc), :]
        send(('ag', arr, chunk, 3), block, block, ag_ss.at[arr, chunk, 2], ag_rs.at[arr, chunk, 2], 'tp', tp_peer(1))

    def gathered(arr, chunk):
        copies[('ag', arr, chunk, 1)].wait_recv()
        copies[('ag', arr, chunk, 3)].wait_recv()

    for chunk in range(chunks):
        for arr in (grad, feat):
            fulls[arr][chunk, :, chan_rows(me, chan_loc), :] = sources[arr][:, :, chunk * LANES:(chunk + 1) * LANES]
    build_grid_mats(to_ref, fromt_ref, up_mat, dgrid_mat, z_mat, dh_mat, dims['blk_pts'])
    for degree in range(degrees):
        up_t[degree] = up_ref[degree].astype(F32).T.astype(BF16)
        down_t[degree] = down_ref[degree].astype(F32).T.astype(BF16)
    gate_t[...] = gate_ref[...].astype(F32).T.astype(BF16)
    for buf in (ybuf, dmbuf):
        tail = 192
        buf[:, tail:, :] = jnp.zeros((buf.shape[0], KPAD - tail, LANES), BF16)
    wgrad[...] = jnp.zeros_like(wgrad)
    back_src[...] = jnp.zeros_like(back_src)

    def gain_block(tp, rows):
        eye = iota2((chan_loc, chan_loc), 0) == iota2((chan_loc, chan_loc), 1)
        for degree in range(degrees):
            col = jnp.sum(jnp.where(eye, rows[degree:degree + 1, :], 0.0), axis=1, keepdims=True)
            gain_cols[degree, chan_rows(tp, chan_loc), :] = jnp.broadcast_to(col, (chan_loc, LANES))

    gain_block(me, gain_ref[...])

    def grad_part(chunk):
        d_mixed = split_coefs([mm(down_ref[degree], lane_cat(gfull, chunk, degree)) for degree in range(degrees)])
        dm_zero[...] = rounded(d_mixed[0])
        for pair in range((coefs - 1) // 2):
            dmbuf[:, 16 * pair:16 * pair + 16, :] = pair_rows(d_mixed[2 * pair + 1], d_mixed[2 * pair + 2])

        def step(idx, carry):
            rhs = jnp.concatenate([dmbuf[2 * idx], dmbuf[2 * idx + 1]], axis=1)
            for blk in range(blk_count):
                dgbuf[idx, blk] = mm(dgrid_mat[blk], rhs).astype(BF16)
            return carry

        lax.fori_loop(0, steps, step, 0)

    def normalize(chunk):
        scalar = xfull[chunk, 0].astype(F32)
        mean = jnp.sum(scalar, axis=0, keepdims=True) / channels
        centered = scalar - mean
        inv_s = lax.rsqrt(jnp.sum(centered * centered, axis=0, keepdims=True) / channels + NORM_EPS)
        squares = jnp.zeros((channels, LANES), F32)
        for coef in range(1, coefs):
            vec = xfull[chunk, coef].astype(F32)
            squares = squares + vec * vec
        inv_v = lax.rsqrt(jnp.sum(squares, axis=0, keepdims=True) / vec_count + NORM_EPS)
        stat_buf[chunk, 0:1, :] = mean
        stat_buf[chunk, 1:2, :] = inv_s
        stat_buf[chunk, 2:3, :] = inv_v
        nfull[chunk, 0] = (centered * inv_s * gain_cols[0]).astype(BF16)
        for degree in range(1, degrees):
            for coef in degree_span(degree):
                nfull[chunk, coef] = (xfull[chunk, coef].astype(F32) * inv_v * gain_cols[degree]).astype(BF16)

    def hidden_part(chunk):
        hid = split_coefs([mm(up_t[degree], lane_cat(nfull, chunk, degree)) for degree in range(degrees)])
        hid.append(jnp.zeros_like(hid[0]))
        for pair in range((coefs + 1) // 2):
            ybuf[:, 16 * pair:16 * pair + 16, :] = pair_rows(hid[2 * pair], hid[2 * pair + 1])
        half = rounded(mm(gate_t[...], nfull[chunk, 0])) * 0.5
        tan = jnp.tanh(half)
        wide = 1.0 + tan
        act = half * wide
        mbuf[chunk, 0] = act.astype(BF16)
        dpg_buf[chunk] = (dm_zero[...] * (0.5 * (wide + act * (1.0 - tan)))).astype(BF16)

    def grid_step(chunk, idx, carry):
        rhs = jnp.concatenate([ybuf[2 * idx], ybuf[2 * idx + 1]], axis=1)
        z_sum = None
        pad = jnp.zeros((KPAD - blk_rows, 2 * LANES), BF16)
        for blk in range(blk_count):
            half = rounded(mm(up_mat[blk], rhs))
            tan = jnp.tanh(half)
            wide = 1.0 + tan
            act = half * wide
            d_pre = dgbuf[idx, blk].astype(F32) * (wide + act * (1.0 - tan))
            z_add = mm(z_mat[blk], jnp.concatenate([act.astype(BF16), pad], axis=0))
            h_add = mm(dh_mat[blk], jnp.concatenate([d_pre.astype(BF16), pad], axis=0))
            z_sum, h_sum = (z_add, h_add) if z_sum is None else (z_sum + z_add, h_sum + h_add)
        rows = pl.ds(pl.multiple_of(16 * idx, 16), 16)

        def by_coef(value, count):
            value = value[:count * SUB].reshape(count, SUB, 2 * LANES)
            return jnp.concatenate([value[:, :, :LANES], value[:, :, LANES:]], axis=1).astype(BF16)

        mbuf[chunk, 1:coefs, rows, :] = by_coef(z_sum, coefs - 1)
        dhbuf[chunk, :, rows, :] = by_coef(h_sum, coefs)
        return carry

    def grid_part(chunk, first, last):
        lax.fori_loop(first, last, functools.partial(grid_step, chunk), 0)

    def weight_grads(chunk):
        for degree in range(degrees):
            rows = pl.ds(degree * channels, channels)
            wgrad[rows, :] += mm_nt(lane_cat(nfull, chunk, degree), lane_cat(dhbuf, chunk, degree))
            rows = pl.ds((degrees + 1) * channels + degree * hidden, hidden)
            wgrad[rows, :] += mm_nt(lane_cat(mbuf, chunk, degree), lane_cat(gfull, chunk, degree))
        rows = pl.ds(degrees * channels, channels)
        wgrad[rows, :] += mm_nt(nfull[chunk, 0], dpg_buf[chunk])

    def store_part(arr, chunk, per_degree):
        for coef, value in enumerate(split_coefs(per_degree)):
            part[arr, chunk, coef] = value.astype(BF16)

    def input_grads(chunk):
        per_degree = [mm(up_ref[degree], lane_cat(dhbuf, chunk, degree)) for degree in range(degrees)]
        per_degree[0] = per_degree[0] + mm(gate_ref[...], dpg_buf[chunk])
        store_part(dxs, chunk, per_degree)

    def outputs(chunk):
        store_part(outs, chunk, [mm(down_t[degree], lane_cat(mbuf, chunk, degree)) for degree in range(degrees)])

    def scatter_core(arr, chunk):
        for chip in (0, 1):
            rows = chan_rows(2 * chip + 1 - me % 2, chan_loc)
            send(('rs1', arr, chunk, chip), part.at[arr, chunk, :, rows, :], rs1.at[arr, chunk, chip],
                 rs1_ss.at[arr, chunk, chip], rs1_rs.at[arr, chunk, chip], 'tp', tp_peer(1))

    def chip_sum(arr, chunk, chip):
        own = part[arr, chunk, :, chan_rows(2 * chip + me % 2, chan_loc), :].astype(F32)
        return own + rs1[arr, chunk, chip].astype(F32)

    def scatter_chip(arr, chunk):
        for chip in (0, 1):
            copies[('rs1', arr, chunk, chip)].wait_recv()
        rs2_src[arr, chunk] = chip_sum(arr, chunk, 1 - me // 2).astype(BF16)
        send(('rs2', arr, chunk), rs2_src.at[arr, chunk], rs2.at[arr, chunk], rs2_ss.at[arr, chunk], rs2_rs.at[arr, chunk], 'tp', tp_peer(2))

    def scattered(arr, chunk):
        copies[('rs2', arr, chunk)].wait_recv()
        return chip_sum(arr, chunk, me // 2) + rs2[arr, chunk].astype(F32)

    def own_x(chunk):
        return x_ref[:, :, chunk * LANES:(chunk + 1) * LANES].astype(F32)

    def finish_out(chunk):
        out_ref[:, :, chunk * LANES:(chunk + 1) * LANES] = (own_x(chunk) + scattered(outs, chunk)).astype(BF16)

    def own_gain(degree):
        return gain_cols[degree, chan_rows(me, chan_loc), :]

    def back_stats(chunk):
        x_own = own_x(chunk)
        d_norm = rounded(scattered(dxs, chunk))
        rs2[dxs, chunk] = d_norm.astype(BF16)
        d_hat = d_norm[0] * own_gain(0)
        hat = (x_own[0] - stat_buf[chunk, 0:1, :]) * stat_buf[chunk, 1:2, :]
        back_src[chunk, 0:1, :] = jnp.sum(d_hat, axis=0, keepdims=True)
        back_src[chunk, 1:2, :] = jnp.sum(d_hat * hat, axis=0, keepdims=True)
        total = jnp.zeros((chan_loc, LANES), F32)
        for degree in range(1, degrees):
            for coef in degree_span(degree):
                total = total + d_norm[coef] * own_gain(degree) * x_own[coef]
        back_src[chunk, 2:3, :] = jnp.sum(total, axis=0, keepdims=True)
        for hop in (2, 3, 1):
            send(('back', chunk, hop), back_src.at[chunk], back_rx.at[chunk, hop - 1], back_ss.at[chunk, hop - 1], back_rs.at[chunk, hop - 1], 'tp', tp_peer(hop))

    def finish_dx(chunk):
        for hop in (1, 2, 3):
            copies[('back', chunk, hop)].wait_recv()
        sums = (back_src[chunk] + back_rx[chunk, 0]) + (back_rx[chunk, 1] + back_rx[chunk, 2])
        mean, inv_s, inv_v = (stat_buf[chunk, j:j + 1, :] for j in range(3))
        lanes = slice(chunk * LANES, (chunk + 1) * LANES)
        hat = (x_ref[0, :, lanes].astype(F32) - mean) * inv_s
        d_hat = rs2[dxs, chunk, 0].astype(F32) * own_gain(0)
        d_scalar = inv_s * (d_hat - sums[0:1] / channels - hat * (sums[1:2] / channels))
        dx_ref[0, :, lanes] = (d_scalar + g_ref[0, :, lanes].astype(F32)).astype(BF16)
        scale = (inv_v * inv_v * inv_v) * (sums[2:3] / vec_count)
        for degree in range(1, degrees):
            for coef in degree_span(degree):
                d_hat = rs2[dxs, chunk, coef].astype(F32) * own_gain(degree)
                d_vec = inv_v * d_hat - x_ref[coef, :, lanes].astype(F32) * scale
                dx_ref[coef, :, lanes] = (d_vec + g_ref[coef, :, lanes].astype(F32)).astype(BF16)

    def quarter_rows(dp):
        return pl.ds(pl.multiple_of(dp * quarter, 16), quarter)

    def wgrad_scatter():
        for hop in (3, 1, 2):
            send(('w1', hop), wgrad.at[quarter_rows(dp_peer(hop))], wgrad_rx.at[hop - 1], w1_ss.at[hop - 1], w1_rs.at[hop - 1], 'dp', dp_peer(hop))

    def wgrad_reduce():
        for hop in (1, 2, 3):
            copies[('w1', hop)].wait_recv()
        total = (wgrad[quarter_rows(my_dp), :] + wgrad_rx[0]) + (wgrad_rx[1] + wgrad_rx[2])
        wsum[...] = total.astype(BF16)
        wfull[quarter_rows(my_dp), :] = wsum[...]
        for hop in (3, 1, 2):
            send(('w2', hop), wsum, wfull.at[quarter_rows(my_dp)], w2_ss.at[hop - 1], w2_rs.at[hop - 1], 'dp', dp_peer(hop))

    def wgrad_finish():
        for hop in (1, 2, 3):
            copies[('w2', hop)].wait_recv()
        dup_ref[...] = wfull[:degrees * channels, :]
        dgate_ref[...] = wfull[degrees * channels:(degrees + 1) * channels, :]
        ddown_ref[...] = wfull[(degrees + 1) * channels:, :]

    relay(grad, 0)
    for hop in (1, 2, 3):
        copies[('gain', hop)].wait_recv()
        gain_block(tp_peer(hop), gain_rx[hop - 1])
    gathered(grad, 0)
    grad_part(0)
    relay(feat, 0)
    gathered(feat, 0)
    normalize(0)
    hidden_part(0)
    grid_part(0, 0, steps // 2)
    relay(grad, 1)
    grid_part(0, steps // 2, steps)
    weight_grads(0)
    input_grads(0)
    scatter_core(dxs, 0)
    outputs(0)
    scatter_core(outs, 0)
    relay(feat, 1)
    scatter_chip(dxs, 0)
    gathered(grad, 1)
    grad_part(1)
    scatter_chip(outs, 0)
    gathered(feat, 1)
    normalize(1)
    hidden_part(1)
    grid_part(1, 0, steps)
    weight_grads(1)
    wgrad_scatter()
    input_grads(1)
    scatter_core(dxs, 1)
    outputs(1)
    scatter_chip(dxs, 1)
    scatter_core(outs, 1)
    back_stats(0)
    scatter_chip(outs, 1)
    finish_out(0)
    finish_dx(0)
    wgrad_reduce()
    back_stats(1)
    finish_out(1)
    finish_dx(1)
    wgrad_finish()
    for copy in copies.values():
        copy.wait_send()


def solution(mesh):
    act_spec = P('dp', None, 'tp')
    in_specs = (act_spec, P(None, 'tp'), P(None, None, 'tp'), P(None, 'tp'), P(None, 'tp', None), P(None, None), P(None, None), act_spec)
    out_specs = (act_spec, act_spec, P(None, None, 'tp'), P(None, 'tp'), P(None, 'tp', None))

    def local_step(x_loc, gain_loc, up_loc, gate_loc, down_loc, to_grid, from_grid, grad_loc):
        nodes, coefs, chan_loc = x_loc.shape
        degrees, channels, hidden = up_loc.shape
        points = to_grid.shape[1]
        blk_pts = 28
        blks = points // blk_pts
        chunks = nodes // LANES
        groups = hidden // SUB
        w_rows = degrees * channels + channels + degrees * hidden
        dma = pltpu.SemaphoreType.DMA

        def vm(*shape, dtype=BF16):
            return pltpu.VMEM(shape, dtype)

        full = (chunks, coefs, channels, LANES)
        scratch = [
            vm(*full), vm(*full), vm(*full),
            vm(3, degrees, chan_loc, dtype=F32), vm(degrees, channels, LANES, dtype=F32),
            vm(degrees, hidden, channels), vm(degrees, channels, hidden), vm(hidden, channels),
            vm(blks, blk_pts * SUB, KPAD), vm(blks, blk_pts * SUB, KPAD), vm(blks, (coefs - 1) * SUB, KPAD), vm(blks, (coefs + 1) * SUB, KPAD),
            vm(groups, KPAD, LANES), vm(groups, KPAD, LANES), vm(groups // 2, blks, blk_pts * SUB, 2 * LANES),
            vm(hidden, LANES, dtype=F32), vm(chunks, coefs, hidden, LANES), vm(chunks, coefs, hidden, LANES), vm(chunks, hidden, LANES),
            vm(chunks, SUB, LANES, dtype=F32),
            vm(2, *full), vm(2, chunks, 2, coefs, chan_loc, LANES), vm(2, chunks, coefs, chan_loc, LANES), vm(2, chunks, coefs, chan_loc, LANES),
            vm(chunks, SUB, LANES, dtype=F32), vm(chunks, 3, SUB, LANES, dtype=F32),
            vm(w_rows, hidden, dtype=F32), vm(3, w_rows // 4, hidden, dtype=F32), vm(w_rows // 4, hidden), vm(w_rows, hidden),
            dma((2, chunks, 3)), dma((2, chunks, 3)), dma((3,)), dma((3,)),
            dma((2, chunks, 2)), dma((2, chunks, 2)), dma((2, chunks)), dma((2, chunks)),
            dma((chunks, 3)), dma((chunks, 3)), dma((3,)), dma((3,)), dma((3,)), dma((3,)),
        ]
        vmem = pl.BlockSpec(memory_space=pltpu.VMEM)
        act = jax.ShapeDtypeStruct((coefs, chan_loc, nodes), BF16)
        out_t, dx_t, d_up, d_gate, d_down = pl.pallas_call(
            functools.partial(kernel, {'chunks': chunks, 'blk_pts': blk_pts}),
            out_shape=(act, act, jax.ShapeDtypeStruct((degrees * channels, hidden), BF16), jax.ShapeDtypeStruct((channels, hidden), BF16), jax.ShapeDtypeStruct((degrees * hidden, channels), BF16)),
            in_specs=[vmem] * 8,
            out_specs=(vmem,) * 5,
            scratch_shapes=scratch,
            compiler_params=pltpu.CompilerParams(collective_id=0, has_side_effects=True, vmem_limit_bytes=60 * 1024 * 1024),
            name='s2_ffn',
        )(x_loc.transpose(1, 2, 0), grad_loc.transpose(1, 2, 0), gain_loc, up_loc, gate_loc, down_loc, to_grid, from_grid.T)
        return (out_t.transpose(2, 0, 1), dx_t.transpose(2, 0, 1), d_up.reshape(degrees, channels, hidden), d_gate, d_down.reshape(degrees, hidden, channels))

    return jax.shard_map(local_step, mesh=mesh, in_specs=in_specs, out_specs=out_specs, check_vma=False)
```

time: 199 us -> 79.3 us (0.40)
  Pallas kernels: 0 us -> 73.5 us
  matrix products: 52.8 us -> 0 us
  blocking collectives: 48.7 us -> 0 us
  local copies, waits for them, and re-layouts: 43.6 us -> 4.93 us
  waiting for transfers between devices: 30.1 us -> 0 us
  between operations: 14.4 us -> 0.66 us
  other arithmetic: 8.12 us -> 0 us
    pallas_call x0 -> x1, Pallas kernels: none -> 73.5 us  [local_step(): pl.pallas_call(functools.partial(kernel, {'chunks': chunks, 'blk_pts': bl...]
    dot_general x24 -> x0, matrix products: 52.8 us -> none  [the longest x2 21.3 us: hidden_block(): jnp.einsum('ngh,kg->nkh', d_pre_grid, grid_in, preferred_element_type=jnp...]
    psum x3 -> x0, blocking collectives: 48.7 us -> none  [the longest x1 33.6 us: local_step(): d_up = lax.psum(g_up, 'dp').astype(jnp.bfloat16)]
    all_gather x2 -> x0, waiting for transfers between devices: 29.2 us -> none  [the longest x1 16.7 us: local_step(): xn_full = lax.all_gather(xn_loc, 'tp', axis=2, tiled=True)]
    while x46 -> x0, local copies, waits for them, and re-layouts: 18.3 us -> none
    reshape x3 -> x0, local copies, waits for them, and re-layouts: 7.39 us -> none  [the longest x1 3.45 us: hidden_pass(): xn_full.reshape(blk_shape)]
    convert_element_type x6 -> x0, other arithmetic: 4.92 us -> none  [the longest x1 1.89 us: local_step(): out_loc = (x_f + ffn_delta.astype(jnp.float32)).astype(jnp.bfloat16)]
    all_gather x1 -> x0, local copies, waits for them, and re-layouts: 3.67 us -> none  [local_step(): grad_full = lax.all_gather(grad_loc, 'tp', axis=2, tiled=True)]
  transfers between devices with their start and end apart: 4 -> 0, of which waited for: 3 -> 0; matrix products, arithmetic and copies ran while one was open for 9% -> 0% of each run, Pallas kernels for 0% -> 0%
where the time goes in v1:
time: 79.3 us; the launch traced here: 79.1 us
  Pallas kernels  73.5 us (93%)
  local copies, waits for them, and re-layouts  4.93 us (6%)
    pallas_call x1, Pallas kernels, local_step(): pl.pallas_call(functools.partial(kernel, {'chunks': chunks, 'blk_pts': bl...  73.5 us
    unnamed x13, local copies, waits for them, and re-layouts  4.93 us

profile of v1, /device:TPU:0, one launch (start us, length us, event | category | flops | bytes accessed | tf_op | source)
XLA Modules:
  0.0 79.1 jit_solution(2633082834838476709)
XLA Ops:
  0.6 73.5 %s2_ffn.1 = (bf16[25,32,256]{2,1,0:T(8,128)(2,1)}, bf16[25,32,256]{2,1,0:T(8,128)(2,1)}, bf16[640,128]{1,0:T(8,128)(2,1)}, bf16[128,128]{1,0:T(8,128)(2,1)}, bf16[640,128]{1,0:T(8,128)(2,1)}) custom-call(bf16[25,32,256]{2,1,0:T(8,128)(2,1)} %bitcast.7, bf16[25,32,256]{2,1,0:T(8,128)(2,1)} %bitcast.8, f32[5,32]{1,0:T(8,128)} %gain_ref.1, ...), custom_call_target="tpu_custom_call" | custom-call | tf_op jit(solution)/shard_map/s2_ffn/pallas_call | solution.py:459
  74.1 0.0 copy-start
  74.1 1.8 %copy.18 = bf16[256,25,32]{0,2,1:T(8,128)(2,1)} copy(bf16[256,25,32]{0,2,1:T(8,128)(2,1)} %bitcast.10) | data formatting | bytes 819200
  76.0 0.0 copy-done
  76.0 0.0 copy-start.2
  76.0 0.8 copy.19
  76.7 0.3 copy-done.2
  77.0 0.0 copy-start.3
  77.0 0.0 copy-start.1
  77.0 0.7 copy.20
  77.7 0.1 copy-done.3
  77.8 0.6 copy.21
  78.4 0.0 copy-done.1
  78.4 0.7 copy.22
Async XLA Ops:
  74.1 1.8 %copy-start = (bf16[25,32,256]{2,1,0:T(8,128)(2,1)S(1)}, bf16[25,32,256]{2,1,0:T(8,128)(2,1)}, u32[]{:S(2)}) copy-start(bf16[25,32,256]{2,1,0:T(8,128)(2,1)} %get-tuple-element.11) | copy-start | bytes 1228804
  76.0 1.1 %copy-start.2 = (bf16[640,128]{1,0:T(8,128)(2,1)S(1)}, bf16[640,128]{1,0:T(8,128)(2,1)}, u32[]{:S(2)}) copy-start(bf16[640,128]{1,0:T(8,128)(2,1)} %get-tuple-element.12) | copy-start | bytes 491524
  77.0 0.8 copy-start.3
  77.0 1.4 %copy-start.1 = (bf16[640,128]{1,0:T(8,128)(2,1)S(1)}, bf16[640,128]{1,0:T(8,128)(2,1)}, u32[]{:S(2)}) copy-start(bf16[640,128]{1,0:T(8,128)(2,1)} %get-tuple-element.14) | copy-start | bytes 491524

commit v2 on v1

--- a/solution.py
+++ b/solution.py
@@ -82,6 +82,15 @@
     return pl.ds(pl.multiple_of(tp * chan_loc, chan_loc), chan_loc)
 
 
+def load_wide(ref, index):
+    return jnp.concatenate([ref[index + (0,)], ref[index + (1,)]], axis=1)
+
+
+def store_wide(ref, index, value):
+    ref[index + (0,)] = value[:, :LANES]
+    ref[index + (1,)] = value[:, LANES:]
+
+
 def build_grid_mats(to_ref, fromt_ref, up_mat, dgrid_mat, z_mat, dh_mat, blk_pts):
     coefs, points = to_ref.shape
     vecs = fromt_ref.shape[0]
@@ -96,8 +105,8 @@
     from_cols = lax.dot_general(from_b, spread(vecs, (vecs, KPAD), 1), (((0,), (0,)), ((), ())), preferred_element_type=F32)
     to_cols = (to_cols * 0.5).astype(BF16)
     from_cols = (from_cols * 0.5).astype(BF16)
-    to_rows = mm(spread(coefs, (dh_mat.shape[1], coefs), 0), to_b).astype(BF16)
-    from_rows = mm(spread(vecs, (z_mat.shape[1], vecs), 0), from_b).astype(BF16)
+    to_rows = mm(spread(coefs, (dh_mat.shape[2], coefs), 0), to_b).astype(BF16)
+    from_rows = mm(spread(vecs, (z_mat.shape[2], vecs), 0), from_b).astype(BF16)
 
     def diagonal(value):
         same = iota2(value.shape, 0) % SUB == iota2(value.shape, 1) % SUB
@@ -110,10 +119,10 @@
         shape = (points, KPAD)
         col = iota2(shape, 1)
         pick_t = ones_where((col // SUB + first == iota2(shape, 0)) & (col < blk_rows))
-        up_mat[blk] = diagonal(mm(pick, to_cols))
-        dgrid_mat[blk] = diagonal(mm(pick, from_cols))
-        z_mat[blk] = diagonal(mm(from_rows, pick_t))
-        dh_mat[blk] = diagonal(mm(to_rows, pick_t))
+        store_wide(up_mat, (blk,), diagonal(mm(pick, to_cols)))
+        store_wide(dgrid_mat, (blk,), diagonal(mm(pick, from_cols)))
+        store_wide(z_mat, (blk,), diagonal(mm(from_rows, pick_t)))
+        store_wide(dh_mat, (blk,), diagonal(mm(to_rows, pick_t)))
         return carry
 
     lax.fori_loop(0, points // blk_pts, blk_step, 0)
@@ -122,7 +131,7 @@
 def kernel(dims, x_ref, g_ref, gain_ref, up_ref, gate_ref, down_ref, to_ref, fromt_ref,
            out_ref, dx_ref, dup_ref, dgate_ref, ddown_ref,
            xfull, gfull, nfull, gain_rx, gain_cols, up_t, down_t, gate_t,
-           up_mat, dgrid_mat, z_mat, dh_mat, ybuf, dmbuf, dgbuf, dm_zero, mbuf, dhbuf, dpg_buf,
+           up_mat, dgrid_mat, z_mat, dh_mat, ybuf, dmbuf, dgbuf, dm_zero, act_buf, dpre_buf, mbuf, dhbuf, dpg_buf,
            stat_buf, part, rs1, rs2_src, rs2, back_src, back_rx, wgrad, wgrad_rx, wsum, wfull,
            ag_ss, ag_rs, gain_ss, gain_rs, rs1_ss, rs1_rs, rs2_ss, rs2_rs, back_ss, back_rs, w1_ss, w1_rs, w2_ss, w2_rs):
     coefs, chan_loc, _ = x_ref.shape
@@ -132,7 +141,7 @@
     hidden = gate_ref.shape[1]
     chunks = dims['chunks']
     blk_count = up_mat.shape[0]
-    blk_rows = up_mat.shape[1]
+    blk_rows = up_mat.shape[2]
     steps = hidden // SUB // 2
     quarter = wgrad.shape[0] // 4
     me = lax.axis_index('tp')
@@ -203,9 +212,9 @@
             dmbuf[:, 16 * pair:16 * pair + 16, :] = pair_rows(d_mixed[2 * pair + 1], d_mixed[2 * pair + 2])
 
         def step(idx, carry):
-            rhs = jnp.concatenate([dmbuf[2 * idx], dmbuf[2 * idx + 1]], axis=1)
+            rhs = step_rhs(dmbuf, idx)
             for blk in range(blk_count):
-                dgbuf[idx, blk] = mm(dgrid_mat[blk], rhs).astype(BF16)
+                store_wide(dgbuf, (idx, blk), mm(load_wide(dgrid_mat, (blk,)), rhs).astype(BF16))
             return carry
 
         lax.fori_loop(0, steps, step, 0)
@@ -240,31 +249,55 @@
         mbuf[chunk, 0] = act.astype(BF16)
         dpg_buf[chunk] = (dm_zero[...] * (0.5 * (wide + act * (1.0 - tan)))).astype(BF16)
 
-    def grid_step(chunk, idx, carry):
-        rhs = jnp.concatenate([ybuf[2 * idx], ybuf[2 * idx + 1]], axis=1)
-        z_sum = None
+    def grid_front(idx, blk):
+        half = rounded(mm(load_wide(up_mat, (blk,)), step_rhs(ybuf, idx)))
+        tan = jnp.tanh(half)
+        wide = 1.0 + tan
+        act = half * wide
+        d_pre = load_wide(dgbuf, (idx, blk)).astype(F32) * (wide + act * (1.0 - tan))
+        store_wide(act_buf, (blk,), act.astype(BF16))
+        store_wide(dpre_buf, (blk,), d_pre.astype(BF16))
+
+    def step_rhs(ref, idx):
+        return jnp.concatenate([ref[2 * idx], ref[2 * idx + 1]], axis=1)
+
+    def grid_back(blk):
         pad = jnp.zeros((KPAD - blk_rows, 2 * LANES), BF16)
-        for blk in range(blk_count):
-            half = rounded(mm(up_mat[blk], rhs))
-            tan = jnp.tanh(half)
-            wide = 1.0 + tan
-            act = half * wide
-            d_pre = dgbuf[idx, blk].astype(F32) * (wide + act * (1.0 - tan))
-            z_add = mm(z_mat[blk], jnp.concatenate([act.astype(BF16), pad], axis=0))
-            h_add = mm(dh_mat[blk], jnp.concatenate([d_pre.astype(BF16), pad], axis=0))
-            z_sum, h_sum = (z_add, h_add) if z_sum is None else (z_sum + z_add, h_sum + h_add)
+        z_add = mm(load_wide(z_mat, (blk,)), jnp.concatenate([load_wide(act_buf, (blk,)), pad], axis=0))
+        h_add = mm(load_wide(dh_mat, (blk,)), jnp.concatenate([load_wide(dpre_buf, (blk,)), pad], axis=0))
+        return z_add, h_add
+
+    def grid_store(chunk, idx, sums):
         rows = pl.ds(pl.multiple_of(16 * idx, 16), 16)
 
         def by_coef(value, count):
             value = value[:count * SUB].reshape(count, SUB, 2 * LANES)
             return jnp.concatenate([value[:, :, :LANES], value[:, :, LANES:]], axis=1).astype(BF16)
 
-        mbuf[chunk, 1:coefs, rows, :] = by_coef(z_sum, coefs - 1)
-        dhbuf[chunk, :, rows, :] = by_coef(h_sum, coefs)
-        return carry
+        mbuf[chunk, 1:coefs, rows, :] = by_coef(sums[0], coefs - 1)
+        dhbuf[chunk, :, rows, :] = by_coef(sums[1], coefs)
+
+    def grid_both(chunk, idx, front, back):
+        sums = None
+        for blk in range(blk_count):
+            if back:
+                adds = grid_back(blk)
+                sums = adds if sums is None else (sums[0] + adds[0], sums[1] + adds[1])
+            if front:
+                grid_front(idx, blk)
+        if back:
+            grid_store(chunk, idx - 1, sums)
 
     def grid_part(chunk, first, last):
-        lax.fori_loop(first, last, functools.partial(grid_step, chunk), 0)
+        def step(idx, carry):
+            grid_both(chunk, idx, True, True)
+            return carry
+
+        if first == 0:
+            grid_both(chunk, 0, True, False)
+        lax.fori_loop(max(first, 1), last, step, 0)
+        if last == steps:
+            grid_both(chunk, steps, False, True)
 
     def weight_grads(chunk):
         for degree in range(degrees):
@@ -443,9 +476,9 @@
             vm(*full), vm(*full), vm(*full),
             vm(3, degrees, chan_loc, dtype=F32), vm(degrees, channels, LANES, dtype=F32),
             vm(degrees, hidden, channels), vm(degrees, channels, hidden), vm(hidden, channels),
-            vm(blks, blk_pts * SUB, KPAD), vm(blks, blk_pts * SUB, KPAD), vm(blks, (coefs - 1) * SUB, KPAD), vm(blks, (coefs + 1) * SUB, KPAD),
-            vm(groups, KPAD, LANES), vm(groups, KPAD, LANES), vm(groups // 2, blks, blk_pts * SUB, 2 * LANES),
-            vm(hidden, LANES, dtype=F32), vm(chunks, coefs, hidden, LANES), vm(chunks, coefs, hidden, LANES), vm(chunks, hidden, LANES),
+            vm(blks, 2, blk_pts * SUB, LANES), vm(blks, 2, blk_pts * SUB, LANES), vm(blks, 2, (coefs - 1) * SUB, LANES), vm(blks, 2, (coefs + 1) * SUB, LANES),
+            vm(groups, KPAD, LANES), vm(groups, KPAD, LANES), vm(groups // 2, blks, 2, blk_pts * SUB, LANES),
+            vm(hidden, LANES, dtype=F32), vm(blks, 2, blk_pts * SUB, LANES), vm(blks, 2, blk_pts * SUB, LANES), vm(chunks, coefs, hidden, LANES), vm(chunks, coefs, hidden, LANES), vm(chunks, hidden, LANES),
             vm(chunks, SUB, LANES, dtype=F32),
             vm(2, *full), vm(2, chunks, 2, coefs, chan_loc, LANES), vm(2, chunks, coefs, chan_loc, LANES), vm(2, chunks, coefs, chan_loc, LANES),
             vm(chunks, SUB, LANES, dtype=F32), vm(chunks, 3, SUB, LANES, dtype=F32),

time: 79.3 us -> 65.9 us (0.83)
  Pallas kernels: 73.5 us -> 60.1 us
    pallas_call x1, Pallas kernels: 73.5 us -> 60.1 us  [local_step(): pl.pallas_call(functools.partial(kernel, {'chunks': chunks, 'blk_pts': bl...]
where the time goes in v2:
time: 65.9 us; the launch traced here: 65.7 us
  Pallas kernels  60.1 us (91%)
  local copies, waits for them, and re-layouts  4.93 us (7%)
  between operations  0.66 us (1%)
    pallas_call x1, Pallas kernels, local_step(): pl.pallas_call(functools.partial(kernel, {'chunks': chunks, 'blk_pts': bl...  60.1 us
    unnamed x13, local copies, waits for them, and re-layouts  4.93 us

profile of v2, /device:TPU:0, one launch (start us, length us, event | category | flops | bytes accessed | tf_op | source)
XLA Modules:
  0.0 65.7 jit_solution(16094659600972960850)
XLA Ops:
  0.6 60.1 %s2_ffn.1 = (bf16[25,32,256]{2,1,0:T(8,128)(2,1)}, bf16[25,32,256]{2,1,0:T(8,128)(2,1)}, bf16[640,128]{1,0:T(8,128)(2,1)}, bf16[128,128]{1,0:T(8,128)(2,1)}, bf16[640,128]{1,0:T(8,128)(2,1)}) custom-call(bf16[25,32,256]{2,1,0:T(8,128)(2,1)} %bitcast.7, bf16[25,32,256]{2,1,0:T(8,128)(2,1)} %bitcast.8, f32[5,32]{1,0:T(8,128)} %gain_ref.1, ...), custom_call_target="tpu_custom_call" | custom-call | tf_op jit(solution)/shard_map/s2_ffn/pallas_call | solution.py:492
  60.7 0.0 copy-start
  60.7 1.8 %copy.18 = bf16[256,25,32]{0,2,1:T(8,128)(2,1)} copy(bf16[256,25,32]{0,2,1:T(8,128)(2,1)} %bitcast.10) | data formatting | bytes 819200
  62.6 0.0 copy-done
  62.6 0.0 copy-start.2
  62.6 0.8 %copy.19 = bf16[256,25,32]{0,2,1:T(8,128)(2,1)} copy(bf16[256,25,32]{0,2,1:T(8,128)(2,1)S(1)} %bitcast.9) | data formatting | bytes 819200
  63.3 0.3 copy-done.2
  63.6 0.0 copy-start.3
  63.6 0.0 copy-start.1
  63.6 0.7 %copy.20 = bf16[5,128,128]{2,1,0:T(8,128)(2,1)} copy(bf16[5,128,128]{2,1,0:T(8,128)(2,1)S(1)} %bitcast.12) | data formatting | bytes 327680
  64.3 0.1 copy-done.3
  64.4 0.6 copy.21
  65.0 0.0 copy-done.1
  65.0 0.7 %copy.22 = bf16[5,128,128]{2,1,0:T(8,128)(2,1)} copy(bf16[5,128,128]{2,1,0:T(8,128)(2,1)S(1)} %bitcast.11) | data formatting | bytes 327680
Async XLA Ops:
  60.7 1.8 %copy-start = (bf16[25,32,256]{2,1,0:T(8,128)(2,1)S(1)}, bf16[25,32,256]{2,1,0:T(8,128)(2,1)}, u32[]{:S(2)}) copy-start(bf16[25,32,256]{2,1,0:T(8,128)(2,1)} %get-tuple-element.11) | copy-start | bytes 1228804
  62.6 1.1 %copy-start.2 = (bf16[640,128]{1,0:T(8,128)(2,1)S(1)}, bf16[640,128]{1,0:T(8,128)(2,1)}, u32[]{:S(2)}) copy-start(bf16[640,128]{1,0:T(8,128)(2,1)} %get-tuple-element.12) | copy-start | bytes 491524
  63.6 0.8 %copy-start.3 = (bf16[128,128]{1,0:T(8,128)(2,1)S(1)}, bf16[128,128]{1,0:T(8,128)(2,1)}, u32[]{:S(2)}) copy-start(bf16[128,128]{1,0:T(8,128)(2,1)} %get-tuple-element.23) | copy-start | bytes 98308
  63.6 1.4 %copy-start.1 = (bf16[640,128]{1,0:T(8,128)(2,1)S(1)}, bf16[640,128]{1,0:T(8,128)(2,1)}, u32[]{:S(2)}) copy-start(bf16[640,128]{1,0:T(8,128)(2,1)} %get-tuple-element.14) | copy-start | bytes 491524

commit v3 on v2

--- a/solution.py
+++ b/solution.py
@@ -131,8 +131,8 @@
 def kernel(dims, x_ref, g_ref, gain_ref, up_ref, gate_ref, down_ref, to_ref, fromt_ref,
            out_ref, dx_ref, dup_ref, dgate_ref, ddown_ref,
            xfull, gfull, nfull, gain_rx, gain_cols, up_t, down_t, gate_t,
-           up_mat, dgrid_mat, z_mat, dh_mat, ybuf, dmbuf, dgbuf, dm_zero, act_buf, dpre_buf, mbuf, dhbuf, dpg_buf,
-           stat_buf, part, rs1, rs2_src, rs2, back_src, back_rx, wgrad, wgrad_rx, wsum, wfull,
+           up_mat, dgrid_mat, z_mat, dh_mat, ybuf, dmbuf, slope_buf, gate_slope, half_buf, act_buf, dpre_buf, mbuf, dhbuf, dpg_buf,
+           stat_buf, part, rs1, rs2_src, rs2, back_src, back_rx, wdown_acc, wup_acc, wdown_rx, wup_rx, wdown_sum, wup_sum, wdown_full, wup_full,
            ag_ss, ag_rs, gain_ss, gain_rs, rs1_ss, rs1_rs, rs2_ss, rs2_rs, back_ss, back_rs, w1_ss, w1_rs, w2_ss, w2_rs):
     coefs, chan_loc, _ = x_ref.shape
     degrees = gain_ref.shape[0]
@@ -143,7 +143,10 @@
     blk_count = up_mat.shape[0]
     blk_rows = up_mat.shape[2]
     steps = hidden // SUB // 2
-    quarter = wgrad.shape[0] // 4
+    wgrad = (wdown_acc, wup_acc)
+    wgrad_rx = (wdown_rx, wup_rx)
+    wsum = (wdown_sum, wup_sum)
+    wfull = (wdown_full, wup_full)
     me = lax.axis_index('tp')
     my_dp = lax.axis_index('dp')
     sources = (g_ref, x_ref)
@@ -169,7 +172,7 @@
     for hop in (1, 2, 3):
         send(('gain', hop), gain_ref, gain_rx.at[hop - 1], gain_ss.at[hop - 1], gain_rs.at[hop - 1], 'tp', tp_peer(hop))
     for chunk in range(chunks):
-        for arr in (grad, feat):
+        for arr in (feat, grad):
             for hop in (2, 1):
                 send(('ag', arr, chunk, hop), sources[arr].at[:, :, lanes_of(chunk)], fulls[arr].at[chunk, :, chan_rows(me, chan_loc), :],
                      ag_ss.at[arr, chunk, hop - 1], ag_rs.at[arr, chunk, hop - 1], 'tp', tp_peer(hop))
@@ -194,7 +197,8 @@
     for buf in (ybuf, dmbuf):
         tail = 192
         buf[:, tail:, :] = jnp.zeros((buf.shape[0], KPAD - tail, LANES), BF16)
-    wgrad[...] = jnp.zeros_like(wgrad)
+    for acc in wgrad:
+        acc[...] = jnp.zeros_like(acc)
     back_src[...] = jnp.zeros_like(back_src)
 
     def gain_block(tp, rows):
@@ -204,20 +208,6 @@
             gain_cols[degree, chan_rows(tp, chan_loc), :] = jnp.broadcast_to(col, (chan_loc, LANES))
 
     gain_block(me, gain_ref[...])
-
-    def grad_part(chunk):
-        d_mixed = split_coefs([mm(down_ref[degree], lane_cat(gfull, chunk, degree)) for degree in range(degrees)])
-        dm_zero[...] = rounded(d_mixed[0])
-        for pair in range((coefs - 1) // 2):
-            dmbuf[:, 16 * pair:16 * pair + 16, :] = pair_rows(d_mixed[2 * pair + 1], d_mixed[2 * pair + 2])
-
-        def step(idx, carry):
-            rhs = step_rhs(dmbuf, idx)
-            for blk in range(blk_count):
-                store_wide(dgbuf, (idx, blk), mm(load_wide(dgrid_mat, (blk,)), rhs).astype(BF16))
-            return carry
-
-        lax.fori_loop(0, steps, step, 0)
 
     def normalize(chunk):
         scalar = xfull[chunk, 0].astype(F32)
@@ -237,76 +227,112 @@
             for coef in degree_span(degree):
                 nfull[chunk, coef] = (xfull[chunk, coef].astype(F32) * inv_v * gain_cols[degree]).astype(BF16)
 
+    def step_rhs(ref, idx):
+        return jnp.concatenate([ref[2 * idx], ref[2 * idx + 1]], axis=1)
+
+    def silu_pair(half):
+        tan = jnp.tanh(half)
+        wide = 1.0 + tan
+        act = half * wide
+        return act, wide + act * (1.0 - tan)
+
     def hidden_part(chunk):
         hid = split_coefs([mm(up_t[degree], lane_cat(nfull, chunk, degree)) for degree in range(degrees)])
         hid.append(jnp.zeros_like(hid[0]))
         for pair in range((coefs + 1) // 2):
             ybuf[:, 16 * pair:16 * pair + 16, :] = pair_rows(hid[2 * pair], hid[2 * pair + 1])
-        half = rounded(mm(gate_t[...], nfull[chunk, 0])) * 0.5
-        tan = jnp.tanh(half)
-        wide = 1.0 + tan
-        act = half * wide
+        act, slope = silu_pair(rounded(mm(gate_t[...], nfull[chunk, 0])) * 0.5)
         mbuf[chunk, 0] = act.astype(BF16)
-        dpg_buf[chunk] = (dm_zero[...] * (0.5 * (wide + act * (1.0 - tan)))).astype(BF16)
-
-    def grid_front(idx, blk):
-        half = rounded(mm(load_wide(up_mat, (blk,)), step_rhs(ybuf, idx)))
-        tan = jnp.tanh(half)
-        wide = 1.0 + tan
-        act = half * wide
-        d_pre = load_wide(dgbuf, (idx, blk)).astype(F32) * (wide + act * (1.0 - tan))
+        gate_slope[...] = 0.5 * slope
+
+    def grad_part(chunk):
+        d_mixed = split_coefs([mm(down_ref[degree], lane_cat(gfull, chunk, degree)) for degree in range(degrees)])
+        dpg_buf[chunk] = (rounded(d_mixed[0]) * gate_slope[...]).astype(BF16)
+        for pair in range((coefs - 1) // 2):
+            dmbuf[:, 16 * pair:16 * pair + 16, :] = pair_rows(d_mixed[2 * pair + 1], d_mixed[2 * pair + 2])
+
+    def to_points(idx, blk):
+        store_wide(half_buf, (blk,), mm(load_wide(up_mat, (blk,)), step_rhs(ybuf, idx)).astype(BF16))
+
+    def on_points(idx, blk):
+        act, slope = silu_pair(load_wide(half_buf, (blk,)).astype(F32))
         store_wide(act_buf, (blk,), act.astype(BF16))
-        store_wide(dpre_buf, (blk,), d_pre.astype(BF16))
-
-    def step_rhs(ref, idx):
-        return jnp.concatenate([ref[2 * idx], ref[2 * idx + 1]], axis=1)
-
-    def grid_back(blk):
+        store_wide(slope_buf, (idx, blk), slope)
+
+    def grad_points(idx, blk):
+        d_half = rounded(mm(load_wide(dgrid_mat, (blk,)), step_rhs(dmbuf, idx)))
+        store_wide(dpre_buf, (blk,), (d_half * load_wide(slope_buf, (idx, blk))).astype(BF16))
+
+    def from_points(mat, buf, blk):
         pad = jnp.zeros((KPAD - blk_rows, 2 * LANES), BF16)
-        z_add = mm(load_wide(z_mat, (blk,)), jnp.concatenate([load_wide(act_buf, (blk,)), pad], axis=0))
-        h_add = mm(load_wide(dh_mat, (blk,)), jnp.concatenate([load_wide(dpre_buf, (blk,)), pad], axis=0))
-        return z_add, h_add
-
-    def grid_store(chunk, idx, sums):
+        return mm(load_wide(mat, (blk,)), jnp.concatenate([load_wide(buf, (blk,)), pad], axis=0))
+
+    def store_coefs(dst, chunk, first, idx, value):
+        count = coefs - first
+        value = value[:count * SUB].reshape(count, SUB, 2 * LANES)
         rows = pl.ds(pl.multiple_of(16 * idx, 16), 16)
-
-        def by_coef(value, count):
-            value = value[:count * SUB].reshape(count, SUB, 2 * LANES)
-            return jnp.concatenate([value[:, :, :LANES], value[:, :, LANES:]], axis=1).astype(BF16)
-
-        mbuf[chunk, 1:coefs, rows, :] = by_coef(sums[0], coefs - 1)
-        dhbuf[chunk, :, rows, :] = by_coef(sums[1], coefs)
-
-    def grid_both(chunk, idx, front, back):
-        sums = None
+        dst[chunk, first:coefs, rows, :] = jnp.concatenate([value[:, :, :LANES], value[:, :, LANES:]], axis=1).astype(BF16)
+
+    def forward_turn(chunk, idx, front, mid, back):
+        total = None
         for blk in range(blk_count):
             if back:
-                adds = grid_back(blk)
-                sums = adds if sums is None else (sums[0] + adds[0], sums[1] + adds[1])
+                add = from_points(z_mat, act_buf, blk)
+                total = add if total is None else total + add
+            if mid:
+                on_points(idx - 1, blk)
             if front:
-                grid_front(idx, blk)
+                to_points(idx, blk)
         if back:
-            grid_store(chunk, idx - 1, sums)
-
-    def grid_part(chunk, first, last):
-        def step(idx, carry):
-            grid_both(chunk, idx, True, True)
+            store_coefs(mbuf, chunk, 1, idx - 2, total)
+
+    def backward_turn(chunk, idx, front, back):
+        total = None
+        for blk in range(blk_count):
+            if back:
+                add = from_points(dh_mat, dpre_buf, blk)
+                total = add if total is None else total + add
+            if front:
+                grad_points(idx, blk)
+        if back:
+            store_coefs(dhbuf, chunk, 0, idx - 1, total)
+
+    def loop(turn, first, last):
+        def body(idx, carry):
+            turn(idx)
             return carry
 
-        if first == 0:
-            grid_both(chunk, 0, True, False)
-        lax.fori_loop(max(first, 1), last, step, 0)
-        if last == steps:
-            grid_both(chunk, steps, False, True)
-
-    def weight_grads(chunk):
+        lax.fori_loop(first, last, body, 0)
+
+    def forward_grid(chunk, between):
+        full = functools.partial(forward_turn, chunk, front=True, mid=True, back=True)
+        forward_turn(chunk, 0, True, False, False)
+        forward_turn(chunk, 1, True, True, False)
+        loop(full, 2, steps // 2 + 1)
+        between()
+        loop(full, steps // 2 + 1, steps)
+        forward_turn(chunk, steps, False, True, True)
+        forward_turn(chunk, steps + 1, False, False, True)
+
+    def backward_grid(chunk, between):
+        full = functools.partial(backward_turn, chunk, front=True, back=True)
+        backward_turn(chunk, 0, True, False)
+        loop(full, 1, steps // 2 + 1)
+        between()
+        loop(full, steps // 2 + 1, steps)
+        backward_turn(chunk, steps, False, True)
+
+    def down_grads(chunk):
+        for degree in range(degrees):
+            rows = pl.ds(degree * hidden, hidden)
+            wgrad[0][rows, :] += mm_nt(lane_cat(mbuf, chunk, degree), lane_cat(gfull, chunk, degree))
+
+    def up_grads(chunk):
         for degree in range(degrees):
             rows = pl.ds(degree * channels, channels)
-            wgrad[rows, :] += mm_nt(lane_cat(nfull, chunk, degree), lane_cat(dhbuf, chunk, degree))
-            rows = pl.ds((degrees + 1) * channels + degree * hidden, hidden)
-            wgrad[rows, :] += mm_nt(lane_cat(mbuf, chunk, degree), lane_cat(gfull, chunk, degree))
+            wgrad[1][rows, :] += mm_nt(lane_cat(nfull, chunk, degree), lane_cat(dhbuf, chunk, degree))
         rows = pl.ds(degrees * channels, channels)
-        wgrad[rows, :] += mm_nt(nfull[chunk, 0], dpg_buf[chunk])
+        wgrad[1][rows, :] += mm_nt(nfull[chunk, 0], dpg_buf[chunk])
 
     def store_part(arr, chunk, per_degree):
         for coef, value in enumerate(split_coefs(per_degree)):
@@ -382,74 +408,88 @@
                 d_vec = inv_v * d_hat - x_ref[coef, :, lanes].astype(F32) * scale
                 dx_ref[coef, :, lanes] = (d_vec + g_ref[coef, :, lanes].astype(F32)).astype(BF16)
 
-    def quarter_rows(dp):
+    def quarter_rows(group, dp):
+        quarter = wgrad[group].shape[0] // 4
         return pl.ds(pl.multiple_of(dp * quarter, 16), quarter)
 
-    def wgrad_scatter():
+    def wgrad_scatter(group):
         for hop in (3, 1, 2):
-            send(('w1', hop), wgrad.at[quarter_rows(dp_peer(hop))], wgrad_rx.at[hop - 1], w1_ss.at[hop - 1], w1_rs.at[hop - 1], 'dp', dp_peer(hop))
-
-    def wgrad_reduce():
+            send(('w1', group, hop), wgrad[group].at[quarter_rows(group, dp_peer(hop))], wgrad_rx[group].at[hop - 1],
+                 w1_ss.at[group, hop - 1], w1_rs.at[group, hop - 1], 'dp', dp_peer(hop))
+
+    def wgrad_reduce(group):
         for hop in (1, 2, 3):
-            copies[('w1', hop)].wait_recv()
-        total = (wgrad[quarter_rows(my_dp), :] + wgrad_rx[0]) + (wgrad_rx[1] + wgrad_rx[2])
-        wsum[...] = total.astype(BF16)
-        wfull[quarter_rows(my_dp), :] = wsum[...]
+            copies[('w1', group, hop)].wait_recv()
+        mine = quarter_rows(group, my_dp)
+        got = wgrad_rx[group]
+        total = ((wgrad[group][mine, :] + got[0]) + (got[1] + got[2])).astype(BF16)
+        wsum[group][...] = total
+        wfull[group][mine, :] = total
         for hop in (3, 1, 2):
-            send(('w2', hop), wsum, wfull.at[quarter_rows(my_dp)], w2_ss.at[hop - 1], w2_rs.at[hop - 1], 'dp', dp_peer(hop))
-
-    def wgrad_finish():
+            send(('w2', group, hop), wsum[group], wfull[group].at[mine], w2_ss.at[group, hop - 1], w2_rs.at[group, hop - 1], 'dp', dp_peer(hop))
+
+    def wgrad_finish(group):
         for hop in (1, 2, 3):
-            copies[('w2', hop)].wait_recv()
-        dup_ref[...] = wfull[:degrees * channels, :]
-        dgate_ref[...] = wfull[degrees * channels:(degrees + 1) * channels, :]
-        ddown_ref[...] = wfull[(degrees + 1) * channels:, :]
-
-    relay(grad, 0)
+            copies[('w2', group, hop)].wait_recv()
+        if group == 0:
+            ddown_ref[...] = wfull[0][...]
+        else:
+            dup_ref[...] = wfull[1][:degrees * channels, :]
+            dgate_ref[...] = wfull[1][degrees * channels:, :]
+
+    relay(feat, 0)
     for hop in (1, 2, 3):
         copies[('gain', hop)].wait_recv()
         gain_block(tp_peer(hop), gain_rx[hop - 1])
-    gathered(grad, 0)
-    grad_part(0)
-    relay(feat, 0)
     gathered(feat, 0)
     normalize(0)
     hidden_part(0)
-    grid_part(0, 0, steps // 2)
-    relay(grad, 1)
-    grid_part(0, steps // 2, steps)
-    weight_grads(0)
+    forward_grid(0, lambda: relay(grad, 0))
+    outputs(0)
+    scatter_core(outs, 0)
+    gathered(grad, 0)
+    grad_part(0)
+    scatter_chip(outs, 0)
+    backward_grid(0, lambda: relay(feat, 1))
     input_grads(0)
     scatter_core(dxs, 0)
-    outputs(0)
-    scatter_core(outs, 0)
-    relay(feat, 1)
+    down_grads(0)
+    up_grads(0)
     scatter_chip(dxs, 0)
-    gathered(grad, 1)
-    grad_part(1)
-    scatter_chip(outs, 0)
     gathered(feat, 1)
     normalize(1)
     hidden_part(1)
-    grid_part(1, 0, steps)
-    weight_grads(1)
-    wgrad_scatter()
+    forward_grid(1, lambda: relay(grad, 1))
+    outputs(1)
+    scatter_core(outs, 1)
+    gathered(grad, 1)
+    grad_part(1)
+    down_grads(1)
+    wgrad_scatter(0)
+    scatter_chip(outs, 1)
+    finish_out(0)
+    backward_grid(1, lambda: back_stats(0))
     input_grads(1)
     scatter_core(dxs, 1)
-    outputs(1)
+    up_grads(1)
+    wgrad_scatter(1)
     scatter_chip(dxs, 1)
-    scatter_core(outs, 1)
-    back_stats(0)
-    scatter_chip(outs, 1)
-    finish_out(0)
+    wgrad_reduce(0)
     finish_dx(0)
-    wgrad_reduce()
+    finish_out(1)
+    wgrad_reduce(1)
     back_stats(1)
-    finish_out(1)
+    wgrad_finish(0)
     finish_dx(1)
-    wgrad_finish()
+    wgrad_finish(1)
     for copy in copies.values():
         copy.wait_send()
+
+
+def hand_on(*refs):
+    count = len(refs) // 2
+    for src, dst in zip(refs[:count], refs[count:]):
+        dst[...] = src[...]
 
 
 def solution(mesh):
@@ -465,39 +505,51 @@
         blks = points // blk_pts
         chunks = nodes // LANES
         groups = hidden // SUB
-        w_rows = degrees * channels + channels + degrees * hidden
+        down_rows = degrees * hidden
+        up_rows = degrees * channels + channels
         dma = pltpu.SemaphoreType.DMA
 
         def vm(*shape, dtype=BF16):
             return pltpu.VMEM(shape, dtype)
 
         full = (chunks, coefs, channels, LANES)
+        ins = (x_loc.transpose(1, 2, 0), grad_loc.transpose(1, 2, 0), gain_loc, up_loc, gate_loc, down_loc, to_grid, from_grid.T)
         scratch = [
             vm(*full), vm(*full), vm(*full),
             vm(3, degrees, chan_loc, dtype=F32), vm(degrees, channels, LANES, dtype=F32),
             vm(degrees, hidden, channels), vm(degrees, channels, hidden), vm(hidden, channels),
             vm(blks, 2, blk_pts * SUB, LANES), vm(blks, 2, blk_pts * SUB, LANES), vm(blks, 2, (coefs - 1) * SUB, LANES), vm(blks, 2, (coefs + 1) * SUB, LANES),
-            vm(groups, KPAD, LANES), vm(groups, KPAD, LANES), vm(groups // 2, blks, 2, blk_pts * SUB, LANES),
-            vm(hidden, LANES, dtype=F32), vm(blks, 2, blk_pts * SUB, LANES), vm(blks, 2, blk_pts * SUB, LANES), vm(chunks, coefs, hidden, LANES), vm(chunks, coefs, hidden, LANES), vm(chunks, hidden, LANES),
+            vm(groups, KPAD, LANES), vm(groups, KPAD, LANES), vm(groups // 2, blks, 2, blk_pts * SUB, LANES, dtype=F32),
+            vm(hidden, LANES, dtype=F32), vm(blks, 2, blk_pts * SUB, LANES), vm(blks, 2, blk_pts * SUB, LANES), vm(blks, 2, blk_pts * SUB, LANES), vm(chunks, coefs, hidden, LANES), vm(chunks, coefs, hidden, LANES), vm(chunks, hidden, LANES),
             vm(chunks, SUB, LANES, dtype=F32),
             vm(2, *full), vm(2, chunks, 2, coefs, chan_loc, LANES), vm(2, chunks, coefs, chan_loc, LANES), vm(2, chunks, coefs, chan_loc, LANES),
             vm(chunks, SUB, LANES, dtype=F32), vm(chunks, 3, SUB, LANES, dtype=F32),
-            vm(w_rows, hidden, dtype=F32), vm(3, w_rows // 4, hidden, dtype=F32), vm(w_rows // 4, hidden), vm(w_rows, hidden),
+            vm(down_rows, LANES, dtype=F32), vm(up_rows, LANES, dtype=F32), vm(3, down_rows // 4, LANES, dtype=F32), vm(3, up_rows // 4, LANES, dtype=F32),
+            vm(down_rows // 4, LANES), vm(up_rows // 4, LANES), vm(down_rows, LANES), vm(up_rows, LANES),
             dma((2, chunks, 3)), dma((2, chunks, 3)), dma((3,)), dma((3,)),
             dma((2, chunks, 2)), dma((2, chunks, 2)), dma((2, chunks)), dma((2, chunks)),
-            dma((chunks, 3)), dma((chunks, 3)), dma((3,)), dma((3,)), dma((3,)), dma((3,)),
+            dma((chunks, 3)), dma((chunks, 3)), dma((2, 3)), dma((2, 3)), dma((2, 3)), dma((2, 3)),
         ]
         vmem = pl.BlockSpec(memory_space=pltpu.VMEM)
         act = jax.ShapeDtypeStruct((coefs, chan_loc, nodes), BF16)
-        out_t, dx_t, d_up, d_gate, d_down = pl.pallas_call(
+        shapes = (act, act, jax.ShapeDtypeStruct((degrees * channels, hidden), BF16), jax.ShapeDtypeStruct((channels, hidden), BF16), jax.ShapeDtypeStruct((degrees * hidden, channels), BF16))
+        results = pl.pallas_call(
             functools.partial(kernel, {'chunks': chunks, 'blk_pts': blk_pts}),
-            out_shape=(act, act, jax.ShapeDtypeStruct((degrees * channels, hidden), BF16), jax.ShapeDtypeStruct((channels, hidden), BF16), jax.ShapeDtypeStruct((degrees * hidden, channels), BF16)),
-            in_specs=[vmem] * 8,
+            out_shape=shapes,
+            in_specs=[vmem] * len(ins),
             out_specs=(vmem,) * 5,
             scratch_shapes=scratch,
-            compiler_params=pltpu.CompilerParams(collective_id=0, has_side_effects=True, vmem_limit_bytes=60 * 1024 * 1024),
+            compiler_params=pltpu.CompilerParams(collective_id=0, has_side_effects=True, vmem_limit_bytes=62 * 1024 * 1024),
             name='s2_ffn',
-        )(x_loc.transpose(1, 2, 0), grad_loc.transpose(1, 2, 0), gain_loc, up_loc, gate_loc, down_loc, to_grid, from_grid.T)
+        )(*ins)
+        out_t, dx_t, d_up, d_gate, d_down = pl.pallas_call(
+            hand_on,
+            out_shape=shapes,
+            in_specs=[vmem] * 5,
+            out_specs=(vmem,) * 5,
+            compiler_params=pltpu.CompilerParams(vmem_limit_bytes=62 * 1024 * 1024),
+            name='hand_on',
+        )(*results)
         return (out_t.transpose(2, 0, 1), dx_t.transpose(2, 0, 1), d_up.reshape(degrees, channels, hidden), d_gate, d_down.reshape(degrees, hidden, channels))
 
     return jax.shard_map(local_step, mesh=mesh, in_specs=in_specs, out_specs=out_specs, check_vma=False)

time: 65.9 us -> 59.3 us (0.90)
  local copies, waits for them, and re-layouts: 4.93 us -> 0 us
  Pallas kernels: 60.1 us -> 58.5 us
    unnamed x13 -> x0, local copies, waits for them, and re-layouts: 4.93 us -> none
    pallas_call x1, Pallas kernels: 60.1 us -> 56.2 us  [local_step(): pl.pallas_call(functools.partial(kernel, {'chunks': chunks, 'blk_pts': bl...]
    pallas_call x0 -> x1, Pallas kernels: none -> 2.26 us  [local_step(): pl.pallas_call(hand_on, out_shape=shapes, in_specs=[vmem] * 5, out_specs=...]
where the time goes in v3:
time: 59.3 us; the launch traced here: 59.1 us
  Pallas kernels  58.5 us (99%)
  between operations  0.64 us (1%)
    pallas_call x1, Pallas kernels, local_step(): pl.pallas_call(functools.partial(kernel, {'chunks': chunks, 'blk_pts': bl...  56.2 us
    pallas_call x1, Pallas kernels, local_step(): pl.pallas_call(hand_on, out_shape=shapes, in_specs=[vmem] * 5, out_specs=...  2.26 us

profile of v3, /device:TPU:0, one launch (start us, length us, event | category | flops | bytes accessed | tf_op | source)
XLA Modules:
  0.0 59.1 jit_solution(8443337885703108748)
XLA Ops:
  0.6 56.2 %s2_ffn.1 = (bf16[25,32,256]{2,1,0:T(8,128)(2,1)}, bf16[25,32,256]{2,1,0:T(8,128)(2,1)}, bf16[640,128]{1,0:T(8,128)(2,1)}, bf16[128,128]{1,0:T(8,128)(2,1)}, bf16[640,128]{1,0:T(8,128)(2,1)}) custom-call(bf16[25,32,256]{2,1,0:T(8,128)(2,1)} %bitcast.7, bf16[25,32,256]{2,1,0:T(8,128)(2,1)} %bitcast.8, f32[5,32]{1,0:T(8,128)} %gain_ref.1, ...), custom_call_target="tpu_custom_call" | custom-call | tf_op jit(solution)/shard_map/s2_ffn/pallas_call | solution.py:536
  56.9 2.3 %hand_on.1 = (bf16[25,32,256]{2,1,0:T(8,128)(2,1)}, bf16[25,32,256]{2,1,0:T(8,128)(2,1)}, bf16[640,128]{1,0:T(8,128)(2,1)}, bf16[128,128]{1,0:T(8,128)(2,1)}, bf16[640,128]{1,0:T(8,128)(2,1)}) custom-call(bf16[25,32,256]{2,1,0:T(8,128)(2,1)} %get-tuple-element.15.refs_0_, bf16[25,32,256]{2,1,0:T(8,128)(2,1)} %get-tuple-element.16.refs_1_, ...), custom_call_target="tpu_custom_call" | custom-call | tf_op jit(solution)/shard_map/hand_on/pallas_call | solution.py:545

commit v4 on v3

--- a/solution.py
+++ b/solution.py
@@ -128,11 +128,11 @@
     lax.fori_loop(0, points // blk_pts, blk_step, 0)
 
 
-def kernel(dims, x_ref, g_ref, gain_ref, up_ref, gate_ref, down_ref, to_ref, fromt_ref,
+def kernel(dims, x_hbm, g_hbm, gain_hbm, up_hbm, gate_hbm, down_hbm, to_hbm, fromt_hbm,
            out_ref, dx_ref, dup_ref, dgate_ref, ddown_ref,
-           xfull, gfull, nfull, gain_rx, gain_cols, up_t, down_t, gate_t,
+           x_ref, g_ref, gain_ref, up_ref, gate_ref, down_ref, to_ref, fromt_ref, in_sem, xfull, gfull, nfull, gain_rx, gain_cols, up_t, down_t, gate_t,
            up_mat, dgrid_mat, z_mat, dh_mat, ybuf, dmbuf, slope_buf, gate_slope, half_buf, act_buf, dpre_buf, mbuf, dhbuf, dpg_buf,
-           stat_buf, part, rs1, rs2_src, rs2, back_src, back_rx, wdown_acc, wup_acc, wdown_rx, wup_rx, wdown_sum, wup_sum, wdown_full, wup_full,
+           stat_buf, part, rs1, rs2_src, rs2, back_src, back_rx, wdown_acc, wup0_acc, wup1_acc, wdown_rx, wup0_rx, wup1_rx, wdown_sum, wup0_sum, wup1_sum, wdown_full, wup0_full, wup1_full,
            ag_ss, ag_rs, gain_ss, gain_rs, rs1_ss, rs1_rs, rs2_ss, rs2_rs, back_ss, back_rs, w1_ss, w1_rs, w2_ss, w2_rs):
     coefs, chan_loc, _ = x_ref.shape
     degrees = gain_ref.shape[0]
@@ -143,10 +143,10 @@
     blk_count = up_mat.shape[0]
     blk_rows = up_mat.shape[2]
     steps = hidden // SUB // 2
-    wgrad = (wdown_acc, wup_acc)
-    wgrad_rx = (wdown_rx, wup_rx)
-    wsum = (wdown_sum, wup_sum)
-    wfull = (wdown_full, wup_full)
+    wgrad = (wdown_acc, wup0_acc, wup1_acc)
+    wgrad_rx = (wdown_rx, wup0_rx, wup1_rx)
+    wsum = (wdown_sum, wup0_sum, wup1_sum)
+    wfull = (wdown_full, wup0_full, wup1_full)
     me = lax.axis_index('tp')
     my_dp = lax.axis_index('dp')
     sources = (g_ref, x_ref)
@@ -167,6 +167,13 @@
     for hop in (1, 2, 3):
         pl.semaphore_signal(barrier, inc=1, device_id={'tp': tp_peer(hop)}, device_id_type=MESH)
         pl.semaphore_signal(barrier, inc=1, device_id={'dp': dp_peer(hop)}, device_id_type=MESH)
+    loads = []
+    pairs = ((x_hbm, x_ref), (g_hbm, g_ref), (gain_hbm, gain_ref), (up_hbm, up_ref), (gate_hbm, gate_ref), (down_hbm, down_ref), (to_hbm, to_ref), (fromt_hbm, fromt_ref))
+    for j, (src, dst) in enumerate(pairs):
+        loads.append(pltpu.make_async_copy(src, dst, in_sem.at[j]))
+        loads[j].start()
+    for j in (0, 1, 2):
+        loads[j].wait()
     pl.semaphore_wait(barrier, 6)
 
     for hop in (1, 2, 3):
@@ -186,6 +193,8 @@
         copies[('ag', arr, chunk, 1)].wait_recv()
         copies[('ag', arr, chunk, 3)].wait_recv()
 
+    for load in loads[3:]:
+        load.wait()
     for chunk in range(chunks):
         for arr in (grad, feat):
             fulls[arr][chunk, :, chan_rows(me, chan_loc), :] = sources[arr][:, :, chunk * LANES:(chunk + 1) * LANES]
@@ -327,12 +336,16 @@
             rows = pl.ds(degree * hidden, hidden)
             wgrad[0][rows, :] += mm_nt(lane_cat(mbuf, chunk, degree), lane_cat(gfull, chunk, degree))
 
-    def up_grads(chunk):
+    def up_grads(chunk, half):
+        rows = slice(half * hidden // 2, (half + 1) * hidden // 2)
+        mats = []
         for degree in range(degrees):
-            rows = pl.ds(degree * channels, channels)
-            wgrad[1][rows, :] += mm_nt(lane_cat(nfull, chunk, degree), lane_cat(dhbuf, chunk, degree))
-        rows = pl.ds(degrees * channels, channels)
-        wgrad[1][rows, :] += mm_nt(nfull[chunk, 0], dpg_buf[chunk])
+            d_hid = [dhbuf[chunk, coef, rows, :] for coef in degree_span(degree)]
+            d_hid = d_hid[0] if len(d_hid) == 1 else jnp.concatenate(d_hid, axis=1)
+            mats.append(mm_nt(lane_cat(nfull, chunk, degree), d_hid))
+        mats.append(mm_nt(nfull[chunk, 0], dpg_buf[chunk, rows, :]))
+        for pair in range(len(mats) // 2):
+            wgrad[1 + half][pl.ds(pair * channels, channels), :] += jnp.concatenate(mats[2 * pair:2 * pair + 2], axis=1)
 
     def store_part(arr, chunk, per_degree):
         for coef, value in enumerate(split_coefs(per_degree)):
@@ -431,11 +444,17 @@
     def wgrad_finish(group):
         for hop in (1, 2, 3):
             copies[('w2', group, hop)].wait_recv()
-        if group == 0:
-            ddown_ref[...] = wfull[0][...]
-        else:
-            dup_ref[...] = wfull[1][:degrees * channels, :]
-            dgate_ref[...] = wfull[1][degrees * channels:, :]
+
+    def wgrad_store():
+        ddown_ref[...] = wfull[0][...]
+        for mat in range(degrees + 1):
+            rows = slice(mat // 2 * channels, (mat // 2 + 1) * channels)
+            lanes = slice(mat % 2 * hidden // 2, (mat % 2 + 1) * hidden // 2)
+            value = jnp.concatenate([wfull[1][rows, lanes], wfull[2][rows, lanes]], axis=1)
+            if mat < degrees:
+                dup_ref[mat * channels:(mat + 1) * channels, :] = value
+            else:
+                dgate_ref[...] = value
 
     relay(feat, 0)
     for hop in (1, 2, 3):
@@ -449,15 +468,20 @@
     scatter_core(outs, 0)
     gathered(grad, 0)
     grad_part(0)
-    scatter_chip(outs, 0)
-    backward_grid(0, lambda: relay(feat, 1))
+
+    def between_a():
+        scatter_chip(outs, 0)
+        relay(feat, 1)
+
+    backward_grid(0, between_a)
     input_grads(0)
     scatter_core(dxs, 0)
     down_grads(0)
-    up_grads(0)
-    scatter_chip(dxs, 0)
+    up_grads(0, 0)
+    up_grads(0, 1)
     gathered(feat, 1)
     normalize(1)
+    scatter_chip(dxs, 0)
     hidden_part(1)
     forward_grid(1, lambda: relay(grad, 1))
     outputs(1)
@@ -467,21 +491,29 @@
     down_grads(1)
     wgrad_scatter(0)
     scatter_chip(outs, 1)
-    finish_out(0)
-    backward_grid(1, lambda: back_stats(0))
+
+    def between_b():
+        up_grads(1, 0)
+        wgrad_scatter(1)
+
+    backward_grid(1, between_b)
     input_grads(1)
     scatter_core(dxs, 1)
-    up_grads(1)
-    wgrad_scatter(1)
+    up_grads(1, 1)
+    wgrad_scatter(2)
     scatter_chip(dxs, 1)
     wgrad_reduce(0)
+    wgrad_reduce(1)
+    back_stats(0)
+    finish_out(0)
+    finish_out(1)
+    wgrad_reduce(2)
     finish_dx(0)
-    finish_out(1)
-    wgrad_reduce(1)
     back_stats(1)
-    wgrad_finish(0)
+    for group in range(3):
+        wgrad_finish(group)
+    wgrad_store()
     finish_dx(1)
-    wgrad_finish(1)
     for copy in copies.values():
         copy.wait_send()
 
@@ -505,8 +537,7 @@
         blks = points // blk_pts
         chunks = nodes // LANES
         groups = hidden // SUB
-        down_rows = degrees * hidden
-        up_rows = degrees * channels + channels
+        w_rows = (degrees * hidden, (degrees + 1) * channels // 2, (degrees + 1) * channels // 2)
         dma = pltpu.SemaphoreType.DMA
 
         def vm(*shape, dtype=BF16):
@@ -514,8 +545,8 @@
 
         full = (chunks, coefs, channels, LANES)
         ins = (x_loc.transpose(1, 2, 0), grad_loc.transpose(1, 2, 0), gain_loc, up_loc, gate_loc, down_loc, to_grid, from_grid.T)
-        scratch = [
-            vm(*full), vm(*full), vm(*full),
+        scratch = [vm(*arr.shape, dtype=arr.dtype) for arr in ins] + [
+            dma((len(ins),)), vm(*full), vm(*full), vm(*full),
             vm(3, degrees, chan_loc, dtype=F32), vm(degrees, channels, LANES, dtype=F32),
             vm(degrees, hidden, channels), vm(degrees, channels, hidden), vm(hidden, channels),
             vm(blks, 2, blk_pts * SUB, LANES), vm(blks, 2, blk_pts * SUB, LANES), vm(blks, 2, (coefs - 1) * SUB, LANES), vm(blks, 2, (coefs + 1) * SUB, LANES),
@@ -524,11 +555,11 @@
             vm(chunks, SUB, LANES, dtype=F32),
             vm(2, *full), vm(2, chunks, 2, coefs, chan_loc, LANES), vm(2, chunks, coefs, chan_loc, LANES), vm(2, chunks, coefs, chan_loc, LANES),
             vm(chunks, SUB, LANES, dtype=F32), vm(chunks, 3, SUB, LANES, dtype=F32),
-            vm(down_rows, LANES, dtype=F32), vm(up_rows, LANES, dtype=F32), vm(3, down_rows // 4, LANES, dtype=F32), vm(3, up_rows // 4, LANES, dtype=F32),
-            vm(down_rows // 4, LANES), vm(up_rows // 4, LANES), vm(down_rows, LANES), vm(up_rows, LANES),
+            *(vm(rows, LANES, dtype=F32) for rows in w_rows), *(vm(3, rows // 4, LANES, dtype=F32) for rows in w_rows),
+            *(vm(rows // 4, LANES) for rows in w_rows), *(vm(rows, LANES) for rows in w_rows),
             dma((2, chunks, 3)), dma((2, chunks, 3)), dma((3,)), dma((3,)),
             dma((2, chunks, 2)), dma((2, chunks, 2)), dma((2, chunks)), dma((2, chunks)),
-            dma((chunks, 3)), dma((chunks, 3)), dma((2, 3)), dma((2, 3)), dma((2, 3)), dma((2, 3)),
+            dma((chunks, 3)), dma((chunks, 3)), dma((3, 3)), dma((3, 3)), dma((3, 3)), dma((3, 3)),
         ]
         vmem = pl.BlockSpec(memory_space=pltpu.VMEM)
         act = jax.ShapeDtypeStruct((coefs, chan_loc, nodes), BF16)
@@ -536,7 +567,7 @@
         results = pl.pallas_call(
             functools.partial(kernel, {'chunks': chunks, 'blk_pts': blk_pts}),
             out_shape=shapes,
-            in_specs=[vmem] * len(ins),
+            in_specs=[pl.BlockSpec(memory_space=pl.ANY)] * len(ins),
             out_specs=(vmem,) * 5,
             scratch_shapes=scratch,
             compiler_params=pltpu.CompilerParams(collective_id=0, has_side_effects=True, vmem_limit_bytes=62 * 1024 * 1024),

time: 59.3 us -> 56.8 us (0.958)
  Pallas kernels: 58.5 us -> 56.1 us
    pallas_call x1, Pallas kernels: 56.2 us -> 53.8 us  [local_step(): pl.pallas_call(functools.partial(kernel, {'chunks': chunks, 'blk_pts': bl...]
where the time goes in v4:
time: 56.8 us; the launch traced here: 56.7 us
  Pallas kernels  56.1 us (99%)
  between operations  0.64 us (1%)
    pallas_call x1, Pallas kernels, local_step(): pl.pallas_call(functools.partial(kernel, {'chunks': chunks, 'blk_pts': bl...  53.8 us
    pallas_call x1, Pallas kernels, local_step(): pl.pallas_call(hand_on, out_shape=shapes, in_specs=[vmem] * 5, out_specs=...  2.26 us

profile of v4, /device:TPU:0, one launch (start us, length us, event | category | flops | bytes accessed | tf_op | source)
XLA Modules:
  0.0 56.7 jit_solution(1264518571094069485)
XLA Ops:
  0.6 53.8 %s2_ffn.1 = (bf16[25,32,256]{2,1,0:T(8,128)(2,1)}, bf16[25,32,256]{2,1,0:T(8,128)(2,1)}, bf16[640,128]{1,0:T(8,128)(2,1)}, bf16[128,128]{1,0:T(8,128)(2,1)}, bf16[640,128]{1,0:T(8,128)(2,1)}) custom-call(bf16[25,32,256]{2,1,0:T(8,128)(2,1)} %bitcast.7, bf16[25,32,256]{2,1,0:T(8,128)(2,1)} %bitcast.8, f32[5,32]{1,0:T(8,128)} %gain_hbm.1, ...), custom_call_target="tpu_custom_call" | custom-call | tf_op jit(solution)/shard_map/s2_ffn/pallas_call | solution.py:567
  54.4 2.3 %hand_on.1 = (bf16[25,32,256]{2,1,0:T(8,128)(2,1)}, bf16[25,32,256]{2,1,0:T(8,128)(2,1)}, bf16[640,128]{1,0:T(8,128)(2,1)}, bf16[128,128]{1,0:T(8,128)(2,1)}, bf16[640,128]{1,0:T(8,128)(2,1)}) custom-call(bf16[25,32,256]{2,1,0:T(8,128)(2,1)} %get-tuple-element.15.refs_0_, bf16[25,32,256]{2,1,0:T(8,128)(2,1)} %get-tuple-element.16.refs_1_, ...), custom_call_target="tpu_custom_call" | custom-call | tf_op jit(solution)/shard_map/hand_on/pallas_call | solution.py:576

commit v5 on v4

--- a/solution.py
+++ b/solution.py
@@ -307,28 +307,34 @@
             store_coefs(dhbuf, chunk, 0, idx - 1, total)
 
     def loop(turn, first, last):
-        def body(idx, carry):
-            turn(idx)
+        def body(trip, carry):
+            turn(first + 2 * trip)
+            turn(first + 2 * trip + 1)
             return carry
 
-        lax.fori_loop(first, last, body, 0)
-
-    def forward_grid(chunk, between):
+        lax.fori_loop(0, (last - first) // 2, body, 0)
+
+    def forward_grid(chunk, between, last):
         full = functools.partial(forward_turn, chunk, front=True, mid=True, back=True)
+        split = steps - 4
         forward_turn(chunk, 0, True, False, False)
         forward_turn(chunk, 1, True, True, False)
-        loop(full, 2, steps // 2 + 1)
+        loop(full, 2, split)
         between()
-        loop(full, steps // 2 + 1, steps)
+        loop(full, split, steps)
+        last()
         forward_turn(chunk, steps, False, True, True)
         forward_turn(chunk, steps + 1, False, False, True)
-
-    def backward_grid(chunk, between):
+        backward_turn(chunk, 0, True, False)
+
+    def backward_grid(chunk, between, last):
         full = functools.partial(backward_turn, chunk, front=True, back=True)
-        backward_turn(chunk, 0, True, False)
-        loop(full, 1, steps // 2 + 1)
+        split = steps // 2 + 1
+        loop(full, 1, split)
         between()
-        loop(full, steps // 2 + 1, steps)
+        loop(full, split, steps - 1)
+        last()
+        full(steps - 1)
         backward_turn(chunk, steps, False, True)
 
     def down_grads(chunk):
@@ -359,25 +365,27 @@
     def outputs(chunk):
         store_part(outs, chunk, [mm(down_t[degree], lane_cat(mbuf, chunk, degree)) for degree in range(degrees)])
 
+    chips = (1 - me // 2, me // 2)
+
     def scatter_core(arr, chunk):
-        for chip in (0, 1):
+        for slot, chip in enumerate(chips):
             rows = chan_rows(2 * chip + 1 - me % 2, chan_loc)
-            send(('rs1', arr, chunk, chip), part.at[arr, chunk, :, rows, :], rs1.at[arr, chunk, chip],
-                 rs1_ss.at[arr, chunk, chip], rs1_rs.at[arr, chunk, chip], 'tp', tp_peer(1))
-
-    def chip_sum(arr, chunk, chip):
-        own = part[arr, chunk, :, chan_rows(2 * chip + me % 2, chan_loc), :].astype(F32)
-        return own + rs1[arr, chunk, chip].astype(F32)
+            send(('rs1', arr, chunk, slot), part.at[arr, chunk, :, rows, :], rs1.at[arr, chunk, slot],
+                 rs1_ss.at[arr, chunk, slot], rs1_rs.at[arr, chunk, slot], 'tp', tp_peer(1))
+
+    def chip_sum(arr, chunk, slot):
+        copies[('rs1', arr, chunk, slot)].wait_recv()
+        own = part[arr, chunk, :, chan_rows(2 * chips[slot] + me % 2, chan_loc), :].astype(F32)
+        return own + rs1[arr, chunk, slot].astype(F32)
 
     def scatter_chip(arr, chunk):
-        for chip in (0, 1):
-            copies[('rs1', arr, chunk, chip)].wait_recv()
-        rs2_src[arr, chunk] = chip_sum(arr, chunk, 1 - me // 2).astype(BF16)
+        rs2_src[arr, chunk] = chip_sum(arr, chunk, 0).astype(BF16)
         send(('rs2', arr, chunk), rs2_src.at[arr, chunk], rs2.at[arr, chunk], rs2_ss.at[arr, chunk], rs2_rs.at[arr, chunk], 'tp', tp_peer(2))
 
     def scattered(arr, chunk):
+        total = chip_sum(arr, chunk, 1)
         copies[('rs2', arr, chunk)].wait_recv()
-        return chip_sum(arr, chunk, me // 2) + rs2[arr, chunk].astype(F32)
+        return total + rs2[arr, chunk].astype(F32)
 
     def own_x(chunk):
         return x_ref[:, :, chunk * LANES:(chunk + 1) * LANES].astype(F32)
@@ -463,31 +471,33 @@
     gathered(feat, 0)
     normalize(0)
     hidden_part(0)
-    forward_grid(0, lambda: relay(grad, 0))
+    def arrived(chunk):
+        gathered(grad, chunk)
+        grad_part(chunk)
+
+    forward_grid(0, lambda: relay(grad, 0), lambda: arrived(0))
     outputs(0)
     scatter_core(outs, 0)
-    gathered(grad, 0)
-    grad_part(0)
 
     def between_a():
         scatter_chip(outs, 0)
         relay(feat, 1)
 
-    backward_grid(0, between_a)
+    def last_a():
+        gathered(feat, 1)
+        down_grads(0)
+
+    backward_grid(0, between_a, last_a)
     input_grads(0)
     scatter_core(dxs, 0)
-    down_grads(0)
     up_grads(0, 0)
     up_grads(0, 1)
-    gathered(feat, 1)
     normalize(1)
     scatter_chip(dxs, 0)
     hidden_part(1)
-    forward_grid(1, lambda: relay(grad, 1))
+    forward_grid(1, lambda: relay(grad, 1), lambda: arrived(1))
     outputs(1)
     scatter_core(outs, 1)
-    gathered(grad, 1)
-    grad_part(1)
     down_grads(1)
     wgrad_scatter(0)
     scatter_chip(outs, 1)
@@ -496,7 +506,7 @@
         up_grads(1, 0)
         wgrad_scatter(1)
 
-    backward_grid(1, between_b)
+    backward_grid(1, between_b, lambda: None)
     input_grads(1)
     scatter_core(dxs, 1)
     up_grads(1, 1)
@@ -519,9 +529,17 @@
 
 
 def hand_on(*refs):
-    count = len(refs) // 2
-    for src, dst in zip(refs[:count], refs[count:]):
-        dst[...] = src[...]
+    count = (len(refs) - 2) // 3
+    srcs, dsts, bufs, (in_sem, out_sem) = refs[:count], refs[count:2 * count], refs[2 * count:3 * count], refs[3 * count:]
+    ins = [pltpu.make_async_copy(srcs[j], bufs[j], in_sem.at[j]) for j in range(count)]
+    outs = [pltpu.make_async_copy(bufs[j], dsts[j], out_sem.at[j]) for j in range(count)]
+    for copy in ins:
+        copy.start()
+    for j in range(count):
+        ins[j].wait()
+        outs[j].start()
+    for copy in outs:
+        copy.wait()
 
 
 def solution(mesh):
@@ -576,8 +594,9 @@
         out_t, dx_t, d_up, d_gate, d_down = pl.pallas_call(
             hand_on,
             out_shape=shapes,
-            in_specs=[vmem] * 5,
-            out_specs=(vmem,) * 5,
+            in_specs=[pl.BlockSpec(memory_space=pl.ANY)] * len(shapes),
+            out_specs=(pl.BlockSpec(memory_space=pl.ANY),) * len(shapes),
+            scratch_shapes=[vm(*arr.shape) for arr in shapes] + [dma((len(shapes),)), dma((len(shapes),))],
             compiler_params=pltpu.CompilerParams(vmem_limit_bytes=62 * 1024 * 1024),
             name='hand_on',
         )(*results)

time: 56.8 us -> 54.8 us (0.965)
  Pallas kernels: 56.1 us -> 53.9 us
    pallas_call x1, Pallas kernels: 53.8 us -> 51.8 us  [local_step(): pl.pallas_call(functools.partial(kernel, {'chunks': chunks, 'blk_pts': bl...]
where the time goes in v5:
time: 54.8 us; the launch traced here: 54.7 us
  Pallas kernels  53.9 us (98%)
  between operations  0.8 us (1%)
    pallas_call x1, Pallas kernels, local_step(): pl.pallas_call(functools.partial(kernel, {'chunks': chunks, 'blk_pts': bl...  51.8 us
    pallas_call x1, Pallas kernels, local_step(): pl.pallas_call(hand_on, out_shape=shapes, in_specs=[pl.BlockSpec(memory_s...  2.09 us

profile of v5, /device:TPU:0, one launch (start us, length us, event | category | flops | bytes accessed | tf_op | source)
XLA Modules:
  0.0 54.7 jit_solution(4561662150061509105)
XLA Ops:
  0.6 51.8 %s2_ffn.1 = (bf16[25,32,256]{2,1,0:T(8,128)(2,1)}, bf16[25,32,256]{2,1,0:T(8,128)(2,1)}, bf16[640,128]{1,0:T(8,128)(2,1)}, bf16[128,128]{1,0:T(8,128)(2,1)}, bf16[640,128]{1,0:T(8,128)(2,1)}) custom-call(bf16[25,32,256]{2,1,0:T(8,128)(2,1)} %bitcast.7, bf16[25,32,256]{2,1,0:T(8,128)(2,1)} %bitcast.8, f32[5,32]{1,0:T(8,128)} %gain_hbm.1, ...), custom_call_target="tpu_custom_call" | custom-call | tf_op jit(solution)/shard_map/s2_ffn/pallas_call | solution.py:585
  52.4 2.1 %hand_on.1 = (bf16[25,32,256]{2,1,0:T(8,128)(2,1)}, bf16[25,32,256]{2,1,0:T(8,128)(2,1)}, bf16[640,128]{1,0:T(8,128)(2,1)}, bf16[128,128]{1,0:T(8,128)(2,1)}, bf16[640,128]{1,0:T(8,128)(2,1)}) custom-call(bf16[25,32,256]{2,1,0:T(8,128)(2,1)} %get-tuple-element.15.refs_0_, bf16[25,32,256]{2,1,0:T(8,128)(2,1)} %get-tuple-element.16.refs_1_, ...), custom_call_target="tpu_custom_call" | custom-call | tf_op jit(solution)/shard_map/hand_on/pallas_call | solution.py:594

commit v6 on v5

--- a/solution.py
+++ b/solution.py
@@ -307,12 +307,8 @@
             store_coefs(dhbuf, chunk, 0, idx - 1, total)
 
     def loop(turn, first, last):
-        def body(trip, carry):
-            turn(first + 2 * trip)
-            turn(first + 2 * trip + 1)
-            return carry
-
-        lax.fori_loop(0, (last - first) // 2, body, 0)
+        for idx in range(first, last):
+            turn(idx)
 
     def forward_grid(chunk, between, last):
         full = functools.partial(forward_turn, chunk, front=True, mid=True, back=True)

time: 54.8 us -> 53.8 us (0.982)
  Pallas kernels: 53.9 us -> 52.8 us
    pallas_call x1, Pallas kernels: 51.8 us -> 50.7 us  [local_step(): pl.pallas_call(functools.partial(kernel, {'chunks': chunks, 'blk_pts': bl...]
where the time goes in v6:
time: 53.8 us; the launch traced here: 53.6 us
  Pallas kernels  52.8 us (98%)
  between operations  0.8 us (1%)
    pallas_call x1, Pallas kernels, local_step(): pl.pallas_call(functools.partial(kernel, {'chunks': chunks, 'blk_pts': bl...  50.7 us
    pallas_call x1, Pallas kernels, local_step(): pl.pallas_call(hand_on, out_shape=shapes, in_specs=[pl.BlockSpec(memory_s...  2.09 us

profile of v6, /device:TPU:0, one launch (start us, length us, event | category | flops | bytes accessed | tf_op | source)
XLA Modules:
  0.0 53.6 jit_solution(13077506745695896988)
XLA Ops:
  0.6 50.7 %s2_ffn.1 = (bf16[25,32,256]{2,1,0:T(8,128)(2,1)}, bf16[25,32,256]{2,1,0:T(8,128)(2,1)}, bf16[640,128]{1,0:T(8,128)(2,1)}, bf16[128,128]{1,0:T(8,128)(2,1)}, bf16[640,128]{1,0:T(8,128)(2,1)}) custom-call(bf16[25,32,256]{2,1,0:T(8,128)(2,1)} %bitcast.7, bf16[25,32,256]{2,1,0:T(8,128)(2,1)} %bitcast.8, f32[5,32]{1,0:T(8,128)} %gain_hbm.1, ...), custom_call_target="tpu_custom_call" | custom-call | tf_op jit(solution)/shard_map/s2_ffn/pallas_call | solution.py:581
  51.4 2.1 %hand_on.1 = (bf16[25,32,256]{2,1,0:T(8,128)(2,1)}, bf16[25,32,256]{2,1,0:T(8,128)(2,1)}, bf16[640,128]{1,0:T(8,128)(2,1)}, bf16[128,128]{1,0:T(8,128)(2,1)}, bf16[640,128]{1,0:T(8,128)(2,1)}) custom-call(bf16[25,32,256]{2,1,0:T(8,128)(2,1)} %get-tuple-element.15.refs_0_, bf16[25,32,256]{2,1,0:T(8,128)(2,1)} %get-tuple-element.16.refs_1_, ...), custom_call_target="tpu_custom_call" | custom-call | tf_op jit(solution)/shard_map/hand_on/pallas_call | solution.py:590
